TPU v7x, 128 devices: a whole 4x4x4 slice. The times are simulated.
128 devices in a mesh: gx: 4 (over x_hi, core), gy: 4 (over y), gz: 8 (over z, x_lo).
Axes of the slice: x: 4 (x_hi: 2, x_lo: 2; x = x_hi * 2 + x_lo), y: 4, z: 4, core: 2. Of those that a mesh axis runs over, the one named last changes fastest.
Arguments:
- field: float32 [64, 1024, 1024], P('gx', 'gy', 'gz'), may hold values from -6 to 6
- source: float32 [64, 1024, 1024], P('gx', 'gy', 'gz'), may hold values from -6 to 6
Outputs:
- smoothed: float32 [64, 1024, 1024], P('gx', 'gy', 'gz')
All inputs are finite; a program needn't handle non-finite values.
Results may differ from a plain program's by a relative error of at most 0.00002.
Values sent between devices are 32-bit elements; how exact they have to be, the bound alone decides.
A program may use at most 64 MiB of HBM per device.

v0:
```python
import functools

import jax
import jax.numpy as jnp
from jax import lax
from jax.experimental import pallas as pl
from jax.experimental.pallas import tpu as pltpu
from jax.sharding import PartitionSpec as P

SWEEPS = 3
MESH = pl.DeviceIdType.MESH
GROUP = 32
PAD = 8
X_LO, X_HI, Y_LO, Y_HI, Z_LO, Z_HI = range(6)


def kernel(sizes, f_hbm, s_hbm, ov, fv, sv, x, src, comb, kb, kr, jb, jr, ib, ir, send, recv, fsem, ssem):
    ngx, ngy, ngz = sizes
    planes, rows, cols = f_hbm.shape
    nm = planes // 2
    half = rows // 2
    per_plane = rows // 8
    rounds = 2 * SWEEPS
    gx, gy, gz = (lax.axis_index(a) for a in ("gx", "gy", "gz"))
    has_lo, has_hi = gx > 0, gx < ngx - 1
    one_z = ngz == 2
    y_lo, y_hi = lax.rem(gy + ngy - 1, ngy), lax.rem(gy + 1, ngy)
    z_lo, z_hi = lax.rem(gz + ngz - 1, ngz), lax.rem(gz + 1, ngz)
    order = [m for a in range(nm // 2) for m in (a, nm - 1 - a)]

    def load(ref, to, sem, m):
        return pltpu.make_async_copy(ref.at[pl.ds(2 * m, 2)], to.at[pl.ds(2 * m, 2)], sem.at[m])

    for m in order:
        load(f_hbm, fv, fsem, m).start()
    for m in order:
        load(s_hbm, sv, ssem, m).start()

    barrier = pltpu.get_barrier_semaphore()

    def greet(device):
        pl.semaphore_signal(barrier, inc=1, device_id=device, device_id_type=MESH)

    @pl.when(has_lo)
    def _():
        greet({"gx": gx - 1})

    @pl.when(has_hi)
    def _():
        greet({"gx": gx + 1})

    ys = [y_lo] if ngy == 2 else [y_lo, y_hi]
    zs = [z_lo] if one_z else [z_lo, z_hi]
    for y in ys:
        greet({"gy": y})
    for z in zs:
        greet({"gz": z})

    row8 = lax.broadcasted_iota(jnp.int32, (8, cols), 0)
    lane = lax.broadcasted_iota(jnp.int32, (8, cols), 1)
    odd8 = lax.rem(row8 + lane, 2)
    pair8 = lax.div(lane, 2)
    odd3 = jnp.broadcast_to(odd8[None], (GROUP, 8, cols)) == 1
    first3 = jnp.broadcast_to(lane[None], (GROUP, 8, cols)) == 0
    last3 = jnp.broadcast_to(lane[None], (GROUP, 8, cols)) == cols - 1
    even_lane = lax.rem(lane, 2) == 0
    odd_lane_half = lax.rem(lax.broadcasted_iota(jnp.int32, (half, cols), 1), 2) == 1

    zero = jnp.zeros((rows, cols), jnp.float32)

    @pl.when(jnp.logical_not(has_lo))
    def _():
        for c in range(2):
            x[c, 0, pl.ds(PAD, rows), :] = zero

    @pl.when(jnp.logical_not(has_hi))
    def _():
        for c in range(2):
            x[c, nm + 1, pl.ds(PAD, rows), :] = zero

    def three(v):
        return v.reshape(GROUP, 8, cols)

    def flat(v):
        return v.reshape(GROUP * 8, cols)

    def pair(produce, store, a, pack_to):
        accs = []
        for h, m in enumerate((a, nm - 1 - a)):
            for blk in range(per_plane // GROUP):
                start = blk * GROUP * 8
                y = produce(a, m, h * per_plane + blk * GROUP, start)
                store(m, start, y)
                if pack_to is not None:
                    acc = jnp.zeros((8, cols), jnp.float32)
                    for g in range(GROUP):
                        q = h * per_plane + blk * GROUP + g
                        acc = jnp.where(pair8 == q, pltpu.roll(y[g], (2 * q + 1) % cols, 1), acc)
                    accs.append(acc)
        if pack_to is not None:
            while len(accs) > 1:
                accs = [p + q for p, q in zip(accs[::2], accs[1::2])]
            pack_to[a] = accs[0]

    def copy(src_ref, dst_ref, to, at, out_dir, in_dir):
        return pltpu.make_async_remote_copy(
            src_ref=src_ref, dst_ref=dst_ref, send_sem=send.at[(out_dir, *at)], recv_sem=recv.at[(in_dir, *at)],
            device_id=to, device_id_type=MESH,
        )

    def x_lo_copy(t):
        return copy(ib.at[0, t], ir.at[1, t], {"gx": gx - 1}, (t, 0), X_LO, X_HI)

    def x_hi_copy(t):
        return copy(ib.at[1, t], ir.at[0, t], {"gx": gx + 1}, (t, 0), X_HI, X_LO)

    def y_copies(t, a):
        return (
            copy(jb.at[0, t, a], jr.at[1, t, a], {"gy": y_lo}, (t, a), Y_LO, Y_HI),
            copy(jb.at[1, t, a], jr.at[0, t, a], {"gy": y_hi}, (t, a), Y_HI, Y_LO),
        )

    def z_copies(t, a):
        up = copy(kb.at[t, a], kr.at[0, t, a], {"gz": z_hi}, (t, a), Z_HI, Z_LO)
        if one_z:
            return (up,)
        return (up, copy(kb.at[t, a], kr.at[1, t, a], {"gz": z_lo}, (t, a), Z_LO, Z_HI))

    def face(c, side):
        m = 1 if side == 0 else nm
        even = x[c, m, pl.ds(PAD, half, stride=2), :]
        odd = x[c, m, pl.ds(PAD + 1, half, stride=2), :]
        wanted = c if side == 0 else 1 - c
        return jnp.where(odd_lane_half, even, odd) if wanted == 1 else jnp.where(odd_lane_half, odd, even)

    def send_x(c, t):
        @pl.when(has_lo)
        def _():
            ib[0, t] = face(c, 0)
            x_lo_copy(t).start()

        @pl.when(has_hi)
        def _():
            ib[1, t] = face(c, 1)
            x_hi_copy(t).start()

    def send_yz(c, t, a):
        for z in z_copies(t, a):
            z.start()
        for h, m in enumerate((a, nm - 1 - a)):
            jb[0, t, a, pl.ds(h, 1), :] = x[c, m + 1, pl.ds(PAD, 1), :]
            jb[1, t, a, pl.ds(h, 1), :] = x[c, m + 1, pl.ds(PAD + rows - 1, 1), :]
        for y in y_copies(t, a):
            y.start()

    def take_yz(c, t, a):
        for z in z_copies(t, a):
            z.wait_recv()
        low = kr[0, t, a]
        high = low if one_z else kr[1, t, a]
        comb[a] = jnp.where(even_lane, pltpu.roll(high, cols - 1, 1), pltpu.roll(low, 1, 1))
        for y in y_copies(t, a):
            y.wait_recv()
        for h, m in enumerate((a, nm - 1 - a)):
            x[c, m + 1, pl.ds(PAD - 1, 1), :] = jr[0, t, a, pl.ds(h, 1), :]
            x[c, m + 1, pl.ds(PAD + rows, 1), :] = jr[1, t, a, pl.ds(h, 1), :]

    def take_x(c, t):
        @pl.when(has_lo)
        def _():
            x_hi_copy_in = copy(ib.at[1, t], ir.at[0, t], {"gx": gx - 1}, (t, 0), X_HI, X_LO)
            x_hi_copy_in.wait_recv()
            got = ir[0, t]
            x[c, 0, pl.ds(PAD, half, stride=2), :] = got
            x[c, 0, pl.ds(PAD + 1, half, stride=2), :] = got

        @pl.when(has_hi)
        def _():
            x_lo_copy_in = copy(ib.at[0, t], ir.at[1, t], {"gx": gx + 1}, (t, 0), X_LO, X_HI)
            x_lo_copy_in.wait_recv()
            got = ir[1, t]
            x[c, nm + 1, pl.ds(PAD, half, stride=2), :] = got
            x[c, nm + 1, pl.ds(PAD + 1, half, stride=2), :] = got

    def store_to(c):
        def store(m, start, y):
            x[c, m + 1, pl.ds(PAD + start, GROUP * 8), :] = flat(y)

        return store

    def black_of_field(a, m, q0, start):
        low = three(fv[2 * m, pl.ds(start, GROUP * 8), :])
        high = three(fv[2 * m + 1, pl.ds(start, GROUP * 8), :])
        return jnp.where(odd3, low, high)

    def pack_field(a, carry):
        for m in (a, nm - 1 - a):
            load(f_hbm, fv, fsem, m).wait()
        pair(black_of_field, store_to(1), a, kb.at[0])
        return carry

    def split_source(m, carry):
        for blk in range(per_plane // GROUP):
            rs = pl.ds(blk * GROUP * 8, GROUP * 8)
            low, high = three(sv[2 * m, rs, :]), three(sv[2 * m + 1, rs, :])
            src[0, m, rs, :] = flat(jnp.where(odd3, high, low))
            src[1, m, rs, :] = flat(jnp.where(odd3, low, high))
        return carry

    def split_pair(a, carry):
        for m in (a, nm - 1 - a):
            load(s_hbm, sv, ssem, m).wait()
            split_source(m, 0)
        return carry

    lax.fori_loop(0, nm // 2, pack_field, 0)
    lax.fori_loop(0, nm // 2, split_pair, 0)
    pl.semaphore_wait(barrier, len(ys) + len(zs) + has_lo.astype(jnp.int32) + has_hi.astype(jnp.int32))
    send_x(1, 0)
    for a in range(nm // 2):
        send_yz(1, 0, a)

    def relax(c, t):
        d = 1 - c

        def produce(a, m, q0, start):
            rs = pl.ds(PAD + start, GROUP * 8)
            here = three(x[d, m + 1, rs, :])
            below, above = three(x[d, m, rs, :]), three(x[d, m + 2, rs, :])
            beside = jnp.where(odd3, above, below) if c == 0 else jnp.where(odd3, below, above)
            total = three(src[c, m, pl.ds(start, GROUP * 8), :]) + here + beside
            total = total + three(x[d, m + 1, pl.ds(PAD + start - 1, GROUP * 8), :])
            total = total + three(x[d, m + 1, pl.ds(PAD + start + 1, GROUP * 8), :])
            edges = comb[a]
            edge = jnp.stack(
                [pltpu.roll(edges, (2 * cols - (2 * (q0 + g) + 1)) % cols, 1) for g in range(GROUP)], axis=0
            )
            total = total + jnp.where(first3, edge, pltpu.roll(here, 1, 2))
            total = total + jnp.where(last3, edge, pltpu.roll(here, cols - 1, 2))
            return total * jnp.float32(1.0 / 6.0)

        return produce

    def store_out(m, start, y):
        red = three(x[0, m + 1, pl.ds(PAD + start, GROUP * 8), :])
        rs = pl.ds(start, GROUP * 8)
        ov[2 * m, rs, :] = flat(jnp.where(odd3, y, red))
        ov[2 * m + 1, rs, :] = flat(jnp.where(odd3, red, y))

    for t in range(rounds):
        c = t % 2
        final = t == rounds - 1
        store = store_out if final else store_to(c)
        pack = None if final else kb.at[t + 1]

        def piece(a, first=False):
            take_yz(1 - c, t, a)
            if first:
                take_x(1 - c, t)
            pair(relax(c, t), store, a, pack)
            if not final:
                if first:
                    send_x(c, t + 1)
                send_yz(c, t + 1, a)

        def body(a, carry):
            piece(a)
            return carry

        piece(0, True)
        lax.fori_loop(1, nm // 2, body, 0)

    for t in range(rounds):
        for a in range(nm // 2):
            for cp in z_copies(t, a) + y_copies(t, a):
                cp.wait_send()

        @pl.when(has_lo)
        def _():
            x_lo_copy(t).wait_send()

        @pl.when(has_hi)
        def _():
            x_hi_copy(t).wait_send()


def solution(mesh):
    sizes = tuple(mesh.shape[a] for a in ("gx", "gy", "gz"))

    def on_device(field, source):
        planes, rows, cols = field.shape
        nm, rounds = planes // 2, 2 * SWEEPS
        assert planes % 4 == 0 and rows % (8 * GROUP) == 0 and cols == 128 and rows // 2 == cols
        f32 = jnp.float32
        return pl.pallas_call(
            functools.partial(kernel, sizes),
            out_shape=jax.ShapeDtypeStruct(field.shape, f32),
            in_specs=[pl.BlockSpec(memory_space=pltpu.HBM)] * 2,
            out_specs=pl.BlockSpec(memory_space=pltpu.VMEM),
            scratch_shapes=[
                pltpu.VMEM(field.shape, f32),
                pltpu.VMEM(field.shape, f32),
                pltpu.VMEM((2, nm + 2, rows + 2 * PAD, cols), f32),
                pltpu.VMEM((2, nm, rows, cols), f32),
                pltpu.VMEM((nm // 2, 8, cols), f32),
                pltpu.VMEM((rounds, nm // 2, 8, cols), f32),
                pltpu.VMEM((2, rounds, nm // 2, 8, cols), f32),
                pltpu.VMEM((2, rounds, nm // 2, 2, cols), f32),
                pltpu.VMEM((2, rounds, nm // 2, 2, cols), f32),
                pltpu.VMEM((2, rounds, rows // 2, cols), f32),
                pltpu.VMEM((2, rounds, rows // 2, cols), f32),
                pltpu.SemaphoreType.DMA((6, rounds, nm // 2)),
                pltpu.SemaphoreType.DMA((6, rounds, nm // 2)),
                pltpu.SemaphoreType.DMA((nm,)),
                pltpu.SemaphoreType.DMA((nm,)),
            ],
            compiler_params=pltpu.CompilerParams(
                collective_id=0, has_side_effects=True, vmem_limit_bytes=50 * 1024 * 1024
            ),
        )(field, source)

    spec = P("gx", "gy", "gz")
    return jax.shard_map(on_device, mesh=mesh, in_specs=(spec, spec), out_specs=spec, check_vma=False)
```

profile of v0, /device:TPU:1, one launch (start us, length us, event | category | flops | bytes accessed | tf_op | source)
XLA Modules:
  0.0 41.8 jit_solution(1690073309056855271)
XLA Ops:
  0.0 40.5 %shard_map.28 = f32[16,256,128]{2,1,0:T(8,128)S(1)} custom-call(f32[16,256,128]{2,1,0:T(8,128)} %f_hbm.1, f32[16,256,128]{2,1,0:T(8,128)} %s_hbm.1), custom_call_target="tpu_custom_call" | custom-call | tf_op jit(solution)/shard_map/pallas_call | solution.py:295
  40.5 1.3 %copy.4 = f32[16,256,128]{2,1,0:T(8,128)} copy(f32[16,256,128]{2,1,0:T(8,128)S(1)} %shard_map.28) | data formatting | bytes 4194304
where the time goes:
time: 41.9 us; the launch traced here: 41.8 us
  Pallas kernels  40.5 us (97%)
  local copies, waits for them, and re-layouts  1.32 us (3%)
    pallas_call x1, Pallas kernels, on_device(): pl.pallas_call(functools.partial(kernel, sizes), out_shape=jax.ShapeDtype...  40.5 us
    unnamed x1, local copies, waits for them, and re-layouts  1.32 us

commit v1 on v0

v1 whole, which is shorter than its diff:
```python
import functools

import jax
import jax.numpy as jnp
from jax import lax
from jax.experimental import pallas as pl
from jax.experimental.pallas import tpu as pltpu
from jax.sharding import PartitionSpec as P

SWEEPS = 3
MESH = pl.DeviceIdType.MESH
PAD = 16
OFF = 2
GROUP = 8
THIRD = 1.0 / 6.0


def kernel(sizes, f_hbm, s_hbm, ov, fv, sv, xb, rb, sr, sb, fb, mh, ml, lz, hz, dg, cn, g, rd, sg, cu, cd, ystage, yland, xystage, xyland,
           send, recv, fsem, ssem):
    ngx, ngy, ngz = sizes
    planes, rows, cols = f_hbm.shape
    nm = planes // 2
    blocks = rows // 8
    gx, gy, gz = (lax.axis_index(a) for a in ("gx", "gy", "gz"))
    has_lo, has_hi = gx > 0, gx < ngx - 1
    y_lo, y_hi = lax.rem(gy + ngy - 1, ngy), lax.rem(gy + 1, ngy)
    z_lo, z_hi = lax.rem(gz + ngz - 1, ngz), lax.rem(gz + 1, ngz)
    x_to = (gx - 1, gx + 1)
    y_to = (y_lo, y_hi)
    z_to = (z_lo, z_hi)
    has = (has_lo, has_hi)
    flip = gx >= ngx // 2
    order = [m for a in range(nm // 2) for m in (a, nm - 1 - a)]

    def load(ref, to, sem, m):
        return pltpu.make_async_copy(ref.at[pl.ds(2 * m, 2)], to.at[pl.ds(2 * m, 2)], sem.at[m])

    for m in order:
        load(f_hbm, fv, fsem, m).start()
    for m in order:
        load(s_hbm, sv, ssem, m).start()

    barrier = pltpu.get_barrier_semaphore()

    def greet(device):
        pl.semaphore_signal(barrier, inc=1, device_id=device, device_id_type=MESH)

    for e in range(2):
        greet({"gy": y_to[e]})
        greet({"gz": z_to[e]})
        for d in range(2):
            greet({"gy": y_to[e], "gz": z_to[d]})

        @pl.when(has[e])
        def _():
            greet({"gx": x_to[e]})
            for d in range(2):
                greet({"gx": x_to[e], "gy": y_to[d]})
                greet({"gx": x_to[e], "gz": z_to[d]})

    row8 = lax.broadcasted_iota(jnp.int32, (8, cols), 0)
    lane = lax.broadcasted_iota(jnp.int32, (8, cols), 1)
    off = lax.rem(lane, 4)
    quad = lax.div(lane, 4)
    odd8 = lax.rem(row8 + lane, 2) == 1
    odd_edge = lax.rem(row8 + off, 2) == 0
    first8, last8 = lane == 0, lane == cols - 1

    def rep(mask, n):
        return jnp.broadcast_to(mask[None], (n, 8, cols))

    def roll(v, k):
        k = k % cols
        return v if k == 0 else pltpu.roll(v, k, v.ndim - 1)

    def three(v):
        return v.reshape(v.shape[0] // 8, 8, cols)

    def flat(v):
        return v.reshape(v.shape[0] * 8, cols)

    def pick(parts, y, blk0):
        for k in range(y.shape[0]):
            blk = blk0 + k
            j = blk % len(parts)
            parts[j] = jnp.where(quad == blk, roll(y[k], 4 * blk + 2), parts[j])
        return parts

    def merge(parts):
        while len(parts) > 1:
            parts = [p + q for p, q in zip(parts[::2], parts[1::2])]
        return parts[0]

    zeros8 = jnp.zeros((8, cols), jnp.float32)

    def copy(k, t, src, dst, to, back):
        return pltpu.make_async_remote_copy(
            src_ref=src, dst_ref=dst, send_sem=send.at[k, t], recv_sem=recv.at[back, t], device_id=to, device_id_type=MESH
        )

    def x_copy(t, e, via=None):
        m, to = (0, nm) if e == 0 else (nm - 1, -1)
        return copy(e, t, xb.at[t, OFF + m, pl.ds(PAD, rows)], xb.at[t, OFF + to, pl.ds(PAD, rows)], {"gx": x_to[e if via is None else via]}, 1 - e)

    def y_copy(t, e):
        return copy(2 + e, t, ystage.at[e, t], yland.at[1 - e, t], {"gy": y_to[e]}, 3 - e)

    def z_copy(t, e):
        src, dst = (ml, hz) if e == 0 else (mh, lz)
        return copy(4 + e, t, src.at[t], dst.at[t], {"gz": z_to[e]}, 5 - e)

    def xy_copy(t, e, d, via=None):
        k, back = 6 + 2 * e + d, 6 + 2 * (1 - e) + 1 - d
        return copy(k, t, xystage.at[k - 6, t], xyland.at[back - 6, t], {"gx": x_to[e if via is None else via], "gy": y_to[d]}, back)

    def xz_copy(t, e, d, via=None):
        k, back = 10 + 2 * e + d, 10 + 2 * (1 - e) + 1 - d
        j = 0 if e == 0 else nm // 2 - 1
        return copy(k, t, (ml, mh)[d].at[t, j], dg.at[t, back - 10], {"gx": x_to[e if via is None else via], "gz": z_to[d]}, back)

    def yz_copy(t, e, d):
        k, back = 14 + 2 * e + d, 14 + 2 * (1 - e) + 1 - d
        return copy(k, t, cn.at[1, t, k - 14], cn.at[0, t, back - 14], {"gy": y_to[e], "gz": z_to[d]}, back)

    def sx_copy(e, via=None):
        m, to = (0, nm) if e == 0 else (nm - 1, -1)
        return copy(18 + e, 0, sr.at[OFF + m, pl.ds(PAD, rows)], sr.at[OFF + to, pl.ds(PAD, rows)], {"gx": x_to[e if via is None else via]}, 19 - e)

    def sy_copy(e):
        return copy(20 + e, 0, ystage.at[e, SWEEPS], yland.at[1 - e, SWEEPS], {"gy": y_to[e]}, 21 - e)

    def sz_copy(e):
        src, dst = (ml, hz) if e == 0 else (mh, lz)
        return copy(22 + e, 0, src.at[SWEEPS], dst.at[SWEEPS], {"gz": z_to[e]}, 23 - e)

    def face_copies(t):
        return [y_copy(t, e) for e in range(2)] + [z_copy(t, e) for e in range(2)] + [yz_copy(t, e, d) for e in range(2) for d in range(2)]

    def wall_copies(t, e):
        return [x_copy(t, e)] + [xy_copy(t, e, d) for d in range(2)] + [xz_copy(t, e, d) for d in range(2)]

    def messages(t, src):
        for j in range(nm // 2):
            even, odd = src(2 * j), src(2 * j + 1)
            mh[t, j] = jnp.where(off < 2, even, roll(odd, 2))
            ml[t, j] = jnp.where(off < 2, roll(even, -2), odd)

    def send_all(t):
        for e in range(2):
            r = 0 if e == 0 else 7
            for d in range(2):
                cn[1, t, 2 * e + d] = (ml, mh)[d][t, :, r, :]
        for e in range(2):
            for d in range(2):
                m = 0 if e == 0 else nm - 1
                r = PAD if d == 0 else PAD + rows - 1
                xystage[2 * e + d, t] = xb[t, OFF + m, pl.ds(r, 1), :]
        for e in range(2):
            r = PAD if e == 0 else PAD + rows - 2
            for m in range(nm):
                ystage[e, t, m] = xb[t, OFF + m, pl.ds(r, 2), :]
        for e in range(2):
            for d in range(2):
                yz_copy(t, e, d).start()
        for e in range(2):
            @pl.when(has[e])
            def _():
                for d in range(2):
                    xz_copy(t, e, d).start()
                for d in range(2):
                    xy_copy(t, e, d).start()
        for e in range(2):
            z_copy(t, e).start()
        for e in range(2):
            y_copy(t, e).start()
        for e in range(2):
            @pl.when(has[e])
            def _():
                x_copy(t, e).start()

    def arrive_faces(t):
        for e in range(2):
            z_copy(t, e).wait_recv()
        for e in range(2):
            y_copy(t, e).wait_recv()
        for e in range(2):
            r = PAD - 2 if e == 0 else PAD + rows
            for m in range(nm):
                xb[t, OFF + m, pl.ds(r, 2), :] = yland[e, t, m]
        for j in range(nm // 2):
            low, high = lz[t, j], hz[t, j]
            l1, l3, lm = roll(low, 1), roll(low, 3), roll(low, -1)
            h1, h3, hm = roll(high, 1), roll(high, -3), roll(high, -1)
            g[1 + 2 * j] = jnp.where(off < 2, jnp.where(off == 0, hm, h1), jnp.where(off == 2, l1, l3))
            g[2 + 2 * j] = jnp.where(off < 2, jnp.where(off == 0, h3, hm), jnp.where(off == 2, lm, l1))

    def arrive_diagonals(t):
        for e in range(2):
            for d in range(2):
                yz_copy(t, e, d).wait_recv()
        for j in range(nm // 2):
            for p in range(2):
                a, b = (jnp.broadcast_to(cn[0, t, k, pl.ds(j, 1), :], (8, cols)) for k in (0, 1))
                cu[2 * j + p] = jnp.where(off == 2, roll(a, 5 - 2 * p), roll(b, 5 - 2 * p))
                a, b = (jnp.broadcast_to(cn[0, t, k, pl.ds(j, 1), :], (8, cols)) for k in (2, 3))
                cd[2 * j + p] = jnp.where(off == 2, roll(a, -3 - 2 * p), roll(b, -3 - 2 * p))
        for e in range(2):
            @pl.when(has[e])
            def _():
                for d in range(2):
                    xz_copy(t, 1 - e, d, e).wait_recv()
                    xy_copy(t, 1 - e, d, e).wait_recv()
                i = OFF - 1 if e == 0 else OFF + nm
                for d in range(2):
                    r = PAD - 1 if d == 0 else PAD + rows
                    xb[t, i, pl.ds(r, 1), :] = xyland[2 * e + d, t]
                k = -1 if e == 0 else 1
                g[0 if e == 0 else nm + 1] = jnp.where(off == 2, roll(dg[t, 2 * e], k), roll(dg[t, 2 * e + 1], k))

    def arrive_x(t, late):
        for e in range(2):
            @pl.when(has[e] & (flip if (e == 0) == late else jnp.logical_not(flip)))
            def _():
                x_copy(t, 1 - e, e).wait_recv()

    def edge_red(t):
        for m in range(nm):
            v = g[1 + m]
            up = pltpu.roll(jnp.where(row8 == 7, jnp.where(lane < 4, cu[m], roll(v, 4)), v), 1, 0)
            down = pltpu.roll(jnp.where(row8 == 0, jnp.where(lane >= cols - 4, cd[m], roll(v, -4)), v), 7, 0)
            side = jnp.where(off == 1, roll(v, 1), roll(v, -1))
            beside = jnp.where(odd_edge, g[2 + m], g[m])
            rd[m] = (((sg[m] + v) + (beside + up)) + ((down + side) + fb[t, m])) * jnp.float32(THIRD)

    def relax(read, i, blk0, n, src, edges, c):
        rs = PAD + 8 * blk0
        here = three(read(i, rs, 8 * n))
        below, above = three(read(i - 1, rs, 8 * n)), three(read(i + 1, rs, 8 * n))
        odd = rep(odd8, n)
        beside = jnp.where(odd, above, below) if c == 0 else jnp.where(odd, below, above)
        total = (three(src) + here) + beside
        total = total + three(read(i, rs - 1, 8 * n))
        total = total + three(read(i, rs + 1, 8 * n))
        edge = jnp.stack(edges, axis=0)
        total = total + jnp.where(rep(first8, n), edge, roll(here, 1))
        total = total + jnp.where(rep(last8, n), edge, roll(here, -1))
        return total * jnp.float32(THIRD)

    def red_pair(t, m):
        i = m + OFF

        def read(i, r, n):
            return xb[t, i, pl.ds(r, n), :]

        edges_from = g[m + 1]

        def edge(blk):
            return roll(edges_from, -(4 * blk + 2))

        for blk0 in range(0, blocks, GROUP):
            y = relax(read, i, blk0, GROUP, sr[i, pl.ds(PAD + 8 * blk0, 8 * GROUP), :], [edge(blk0 + k) for k in range(GROUP)], 0)
            rb[i, pl.ds(PAD + 8 * blk0, 8 * GROUP), :] = flat(y)

    def red_rows(t):
        odd = rep(odd8, nm)
        for r, e in ((PAD - 8, [roll(cu[m], -2) for m in range(nm)]), (PAD + rows, [roll(cd[m], 2) for m in range(nm)])):
            def read(i, r):
                return xb[t, pl.ds(i, nm), pl.ds(r, 8), :]

            here = read(OFF, r)
            total = (sr[pl.ds(OFF, nm), pl.ds(r, 8), :] + here) + jnp.where(odd, read(OFF + 1, r), read(OFF - 1, r))
            total = total + read(OFF, r - 1)
            total = total + read(OFF, r + 1)
            edge = jnp.stack(e, axis=0)
            total = total + jnp.where(rep(first8, nm), edge, roll(here, 1))
            total = total + jnp.where(rep(last8, nm), edge, roll(here, -1))
            rb[pl.ds(OFF, nm), pl.ds(r, 8), :] = total * jnp.float32(THIRD)

    def black_pair(m, emit):
        i = m + OFF

        def read(i, r, n):
            return rb[i, pl.ds(r, n), :]

        edges_from = rd[m]
        for blk0 in range(0, blocks, GROUP):
            rs = pl.ds(8 * blk0, 8 * GROUP)
            edges = [roll(edges_from, -(4 * (blk0 + k) + 2)) for k in range(GROUP)]
            emit(blk0, relax(read, i, blk0, GROUP, sb[m, rs, :], edges, 1))

    zero = jnp.zeros((rows + 16, cols), jnp.float32)
    for e in range(2):
        @pl.when(jnp.logical_not(has[e]))
        def _():
            i = OFF - 1 if e == 0 else OFF + nm
            for t in range(SWEEPS):
                xb[t, i, pl.ds(PAD - 8, rows + 16), :] = zero
            rb[i, pl.ds(PAD - 8, rows + 16), :] = zero
            g[0 if e == 0 else nm + 1] = zeros8

    def pack_field(a, carry):
        for m in (a, nm - 1 - a):
            load(f_hbm, fv, fsem, m).wait()
            parts = [zeros8] * 4
            for blk0 in range(0, blocks, GROUP):
                rs = pl.ds(8 * blk0, 8 * GROUP)
                y = jnp.where(rep(odd8, GROUP), three(fv[2 * m, rs, :]), three(fv[2 * m + 1, rs, :]))
                xb[0, OFF + m, pl.ds(PAD + 8 * blk0, 8 * GROUP), :] = flat(y)
                parts = pick(parts, y, blk0)
            fb[0, m] = merge(parts)
        return carry

    def pack_source(a, carry):
        for m in (a, nm - 1 - a):
            load(s_hbm, sv, ssem, m).wait()
            parts = [zeros8] * 4
            for blk0 in range(0, blocks, GROUP):
                rs = pl.ds(8 * blk0, 8 * GROUP)
                low, high = three(sv[2 * m, rs, :]), three(sv[2 * m + 1, rs, :])
                y = jnp.where(rep(odd8, GROUP), high, low)
                sr[OFF + m, pl.ds(PAD + 8 * blk0, 8 * GROUP), :] = flat(y)
                sb[m, rs, :] = flat(jnp.where(rep(odd8, GROUP), low, high))
                parts = pick(parts, y, blk0)
            sg[m] = merge(parts)
        return carry

    lax.fori_loop(0, nm // 2, pack_field, 0)
    messages(0, lambda m: fb[0, m])
    pl.semaphore_wait(barrier, 8 + 5 * (has_lo.astype(jnp.int32) + has_hi.astype(jnp.int32)))
    send_all(0)
    lax.fori_loop(0, nm // 2, pack_source, 0)
    messages(SWEEPS, lambda m: sg[m])
    for e in range(2):
        @pl.when(has[e])
        def _():
            sx_copy(e).start()
        sz_copy(e).start()
        r = PAD if e == 0 else PAD + rows - 1
        for m in range(nm):
            ystage[e, SWEEPS, m, pl.ds(0, 1), :] = sr[OFF + m, pl.ds(r, 1), :]
        sy_copy(e).start()

    for e in range(2):
        sz_copy(e).wait_recv()
        sy_copy(e).wait_recv()
    for e in range(2):
        r = PAD - 1 if e == 0 else PAD + rows
        for m in range(nm):
            sr[OFF + m, pl.ds(r, 1), :] = yland[e, SWEEPS, m, pl.ds(0, 1), :]
    for j in range(nm // 2):
        low, high = lz[SWEEPS, j], hz[SWEEPS, j]
        sg[2 * j] = jnp.where(off == 1, roll(high, 1), roll(low, 1))
        sg[2 * j + 1] = jnp.where(off == 1, roll(high, -1), roll(low, -1))
    for e in range(2):
        @pl.when(has[e])
        def _():
            sx_copy(1 - e, e).wait_recv()

    def at(p):
        return jnp.where(flip, nm - 1 - p, p)

    def half_red(t, p):
        red_pair(t, at(p))

    def halo_red(t, late):
        late = int(late)

        @pl.when((flip & has[1 - late]) | (jnp.logical_not(flip) & has[late]))
        def _():
            red_pair(t, at(nm if late else -1))

    def sweep(t, emitter):
        arrive_faces(t)
        arrive_x(t, False)

        def red_body(p, carry):
            half_red(t, p)
            return carry

        lax.fori_loop(0, nm - 1, red_body, 0)
        arrive_diagonals(t)
        edge_red(t)
        red_rows(t)
        halo_red(t, False)

        def black_body(p, carry):
            emitter(at(p))
            return carry

        lax.fori_loop(0, nm - 2, black_body, 0)
        arrive_x(t, True)
        lax.fori_loop(nm - 1, nm, red_body, 0)
        halo_red(t, True)
        lax.fori_loop(nm - 2, nm, black_body, 0)

    def full(t, carry):
        def emitter(m):
            parts = [zeros8] * 4

            def emit(blk0, y):
                xb[t + 1, OFF + m, pl.ds(PAD + 8 * blk0, 8 * GROUP), :] = flat(y)
                pick(parts, y, blk0)

            black_pair(m, emit)
            fb[t + 1, m] = merge(parts)

        sweep(t, emitter)
        messages(t + 1, lambda m: fb[t + 1, m])
        send_all(t + 1)
        return carry

    lax.fori_loop(0, SWEEPS - 1, full, 0)

    def final(m):
        def emit(blk0, y):
            red = three(rb[OFF + m, pl.ds(PAD + 8 * blk0, 8 * GROUP), :])
            rs = pl.ds(8 * blk0, 8 * GROUP)
            odd = rep(odd8, GROUP)
            ov[2 * m, rs, :] = flat(jnp.where(odd, y, red))
            ov[2 * m + 1, rs, :] = flat(jnp.where(odd, red, y))

        black_pair(m, emit)

    sweep(SWEEPS - 1, final)

    def drain(t, carry):
        for c in face_copies(t):
            c.wait_send()
        for e in range(2):
            @pl.when(has[e])
            def _():
                for c in wall_copies(t, e):
                    c.wait_send()
        return carry

    lax.fori_loop(0, SWEEPS, drain, 0)
    for e in range(2):
        sz_copy(e).wait_send()
        sy_copy(e).wait_send()

        @pl.when(has[e])
        def _():
            sx_copy(e).wait_send()


def solution(mesh):
    sizes = tuple(mesh.shape[a] for a in ("gx", "gy", "gz"))

    def on_device(field, source):
        planes, rows, cols = field.shape
        nm = planes // 2
        assert planes % 4 == 0 and rows == 256 and cols == 128 and rows % (8 * GROUP) == 0
        f32 = jnp.float32
        wide = (nm + 2 * OFF, rows + 2 * PAD, cols)
        return pl.pallas_call(
            functools.partial(kernel, sizes),
            out_shape=jax.ShapeDtypeStruct(field.shape, f32),
            in_specs=[pl.BlockSpec(memory_space=pltpu.HBM)] * 2,
            out_specs=pl.BlockSpec(memory_space=pltpu.VMEM),
            scratch_shapes=[
                pltpu.VMEM(field.shape, f32),
                pltpu.VMEM(field.shape, f32),
                pltpu.VMEM((SWEEPS, *wide), f32),
                pltpu.VMEM(wide, f32),
                pltpu.VMEM(wide, f32),
                pltpu.VMEM((nm, rows, cols), f32),
                pltpu.VMEM((SWEEPS, nm, 8, cols), f32),
                *[pltpu.VMEM((SWEEPS + 1, nm // 2, 8, cols), f32)] * 4,
                pltpu.VMEM((SWEEPS, 4, 8, cols), f32),
                pltpu.VMEM((2, SWEEPS, 4, nm // 2, cols), f32),
                pltpu.VMEM((nm + 2, 8, cols), f32),
                *[pltpu.VMEM((nm, 8, cols), f32)] * 4,
                *[pltpu.VMEM((2, SWEEPS + 1, nm, 2, cols), f32)] * 2,
                *[pltpu.VMEM((4, SWEEPS, 1, cols), f32)] * 2,
                pltpu.SemaphoreType.DMA((24, SWEEPS)),
                pltpu.SemaphoreType.DMA((24, SWEEPS)),
                pltpu.SemaphoreType.DMA((nm,)),
                pltpu.SemaphoreType.DMA((nm,)),
            ],
            compiler_params=pltpu.CompilerParams(
                collective_id=0, has_side_effects=True, vmem_limit_bytes=60 * 1024 * 1024
            ),
        )(field, source)

    spec = P("gx", "gy", "gz")
    return jax.shard_map(on_device, mesh=mesh, in_specs=(spec, spec), out_specs=spec, check_vma=False)
```

time: 41.9 us -> 42 us (level)
  Pallas kernels: 40.5 us -> 38.7 us
  local copies, waits for them, and re-layouts: 1.32 us -> 3.11 us
    unnamed x1, local copies, waits for them, and re-layouts: 1.32 us -> 3.11 us
    pallas_call x1, Pallas kernels: 40.5 us -> 38.7 us  [on_device(): pl.pallas_call(functools.partial(kernel, sizes), out_shape=jax.ShapeDtype...]
where the time goes in v1:
time: 42 us; the launch traced here: 41.9 us
  Pallas kernels  38.7 us (92%)
  local copies, waits for them, and re-layouts  3.11 us (7%)
    pallas_call x1, Pallas kernels, on_device(): pl.pallas_call(functools.partial(kernel, sizes), out_shape=jax.ShapeDtype...  38.7 us
    unnamed x1, local copies, waits for them, and re-layouts  3.11 us

profile of v1, /device:TPU:1, one launch (start us, length us, event | category | flops | bytes accessed | tf_op | source)
XLA Modules:
  0.0 41.9 jit_solution(4947395310687129838)
XLA Ops:
  0.0 38.7 %shard_map.28 = f32[16,256,128]{2,1,0:T(8,128)} custom-call(f32[16,256,128]{2,1,0:T(8,128)} %f_hbm.1, f32[16,256,128]{2,1,0:T(8,128)} %s_hbm.1), custom_call_target="tpu_custom_call" | custom-call | tf_op jit(solution)/shard_map/pallas_call | solution.py:455
  38.7 3.1 %copy.4 = f32[16,256,128]{2,1,0:T(8,128)} copy(f32[16,256,128]{2,1,0:T(8,128)} %shard_map.28) | data formatting | bytes 4194304

commit v2 on v1

--- a/solution.py
+++ b/solution.py
@@ -15,7 +15,7 @@
 THIRD = 1.0 / 6.0
 
 
-def kernel(sizes, f_hbm, s_hbm, ov, fv, sv, xb, rb, sr, sb, fb, mh, ml, lz, hz, dg, cn, g, rd, sg, cu, cd, ystage, yland, xystage, xyland,
+def kernel(sizes, f_hbm, s_hbm, ov, fv, sv, xb, rb, sr, sb, fb, mh, ml, lz, hz, dg, cn, g, rd, sg, cu, cd, ystage, yland, xystage, xyland, sface, sedge,
            send, recv, fsem, ssem):
     ngx, ngy, ngz = sizes
     planes, rows, cols = f_hbm.shape
@@ -123,15 +123,13 @@
         return copy(k, t, cn.at[1, t, k - 14], cn.at[0, t, back - 14], {"gy": y_to[e], "gz": z_to[d]}, back)
 
     def sx_copy(e, via=None):
-        m, to = (0, nm) if e == 0 else (nm - 1, -1)
-        return copy(18 + e, 0, sr.at[OFF + m, pl.ds(PAD, rows)], sr.at[OFF + to, pl.ds(PAD, rows)], {"gx": x_to[e if via is None else via]}, 19 - e)
+        return copy(18 + e, 0, sface.at[0, e], sface.at[1, 1 - e], {"gx": x_to[e if via is None else via]}, 19 - e)
 
     def sy_copy(e):
         return copy(20 + e, 0, ystage.at[e, SWEEPS], yland.at[1 - e, SWEEPS], {"gy": y_to[e]}, 21 - e)
 
     def sz_copy(e):
-        src, dst = (ml, hz) if e == 0 else (mh, lz)
-        return copy(22 + e, 0, src.at[SWEEPS], dst.at[SWEEPS], {"gz": z_to[e]}, 23 - e)
+        return copy(22 + e, 0, sedge.at[0, e], sedge.at[1, 1 - e], {"gz": z_to[e]}, 23 - e)
 
     def face_copies(t):
         return [y_copy(t, e) for e in range(2)] + [z_copy(t, e) for e in range(2)] + [yz_copy(t, e, d) for e in range(2) for d in range(2)]
@@ -329,32 +327,49 @@
     pl.semaphore_wait(barrier, 8 + 5 * (has_lo.astype(jnp.int32) + has_hi.astype(jnp.int32)))
     send_all(0)
     lax.fori_loop(0, nm // 2, pack_source, 0)
-    messages(SWEEPS, lambda m: sg[m])
+    half = rows // 2
+    odd_lane = lax.rem(lax.broadcasted_iota(jnp.int32, (half, cols), 1), 2) == 1
     for e in range(2):
-        @pl.when(has[e])
-        def _():
-            sx_copy(e).start()
+        for j in range(nm // 4):
+            parts = [roll(sg[4 * j + k], k - 2 + e) for k in range(4)]
+            sedge[0, e, j] = jnp.where(off < 2, jnp.where(off == 0, parts[0], parts[1]), jnp.where(off == 2, parts[2], parts[3]))
         sz_copy(e).start()
+    for e in range(2):
         r = PAD if e == 0 else PAD + rows - 1
         for m in range(nm):
             ystage[e, SWEEPS, m, pl.ds(0, 1), :] = sr[OFF + m, pl.ds(r, 1), :]
         sy_copy(e).start()
-
-    for e in range(2):
-        sz_copy(e).wait_recv()
-        sy_copy(e).wait_recv()
-    for e in range(2):
-        r = PAD - 1 if e == 0 else PAD + rows
-        for m in range(nm):
-            sr[OFF + m, pl.ds(r, 1), :] = yland[e, SWEEPS, m, pl.ds(0, 1), :]
-    for j in range(nm // 2):
-        low, high = lz[SWEEPS, j], hz[SWEEPS, j]
-        sg[2 * j] = jnp.where(off == 1, roll(high, 1), roll(low, 1))
-        sg[2 * j + 1] = jnp.where(off == 1, roll(high, -1), roll(low, -1))
     for e in range(2):
         @pl.when(has[e])
         def _():
-            sx_copy(1 - e, e).wait_recv()
+            i = OFF if e == 0 else OFF + nm - 1
+            even = sr[i, pl.ds(PAD, half, stride=2), :]
+            odd = sr[i, pl.ds(PAD + 1, half, stride=2), :]
+            sface[0, e] = jnp.where(odd_lane, odd, even) if e == 0 else jnp.where(odd_lane, even, odd)
+            sx_copy(e).start()
+
+    def take_source():
+        for e in range(2):
+            sz_copy(e).wait_recv()
+            sy_copy(e).wait_recv()
+        for e in range(2):
+            r = PAD - 1 if e == 0 else PAD + rows
+            for m in range(nm):
+                sr[OFF + m, pl.ds(r, 1), :] = yland[e, SWEEPS, m, pl.ds(0, 1), :]
+        for j in range(nm // 4):
+            low, high = sedge[1, 0, j], sedge[1, 1, j]
+            for k in range(4):
+                sg[4 * j + k] = jnp.where(off == 1, roll(high, 1 - k), roll(low, 2 - k))
+
+    def take_source_x(late):
+        for e in range(2):
+            @pl.when(has[e] & (flip if (e == 0) == late else jnp.logical_not(flip)))
+            def _():
+                sx_copy(1 - e, e).wait_recv()
+                i = OFF - 1 if e == 0 else OFF + nm
+                got = sface[1, e]
+                sr[i, pl.ds(PAD, half, stride=2), :] = got
+                sr[i, pl.ds(PAD + 1, half, stride=2), :] = got
 
     def at(p):
         return jnp.where(flip, nm - 1 - p, p)
@@ -369,6 +384,12 @@
         def _():
             red_pair(t, at(nm if late else -1))
 
+    def on_first(t, do):
+        if not isinstance(t, int):
+            pl.when(t == 0)(do)
+        elif t == 0:
+            do()
+
     def sweep(t, emitter):
         arrive_faces(t)
         arrive_x(t, False)
@@ -379,8 +400,10 @@
 
         lax.fori_loop(0, nm - 1, red_body, 0)
         arrive_diagonals(t)
+        on_first(t, take_source)
         edge_red(t)
         red_rows(t)
+        on_first(t, lambda: take_source_x(False))
         halo_red(t, False)
 
         def black_body(p, carry):
@@ -390,6 +413,7 @@
         lax.fori_loop(0, nm - 2, black_body, 0)
         arrive_x(t, True)
         lax.fori_loop(nm - 1, nm, red_body, 0)
+        on_first(t, lambda: take_source_x(True))
         halo_red(t, True)
         lax.fori_loop(nm - 2, nm, black_body, 0)
 
@@ -465,13 +489,15 @@
                 pltpu.VMEM(wide, f32),
                 pltpu.VMEM((nm, rows, cols), f32),
                 pltpu.VMEM((SWEEPS, nm, 8, cols), f32),
-                *[pltpu.VMEM((SWEEPS + 1, nm // 2, 8, cols), f32)] * 4,
+                *[pltpu.VMEM((SWEEPS, nm // 2, 8, cols), f32)] * 4,
                 pltpu.VMEM((SWEEPS, 4, 8, cols), f32),
                 pltpu.VMEM((2, SWEEPS, 4, nm // 2, cols), f32),
                 pltpu.VMEM((nm + 2, 8, cols), f32),
                 *[pltpu.VMEM((nm, 8, cols), f32)] * 4,
                 *[pltpu.VMEM((2, SWEEPS + 1, nm, 2, cols), f32)] * 2,
                 *[pltpu.VMEM((4, SWEEPS, 1, cols), f32)] * 2,
+                pltpu.VMEM((2, 2, rows // 2, cols), f32),
+                pltpu.VMEM((2, 2, nm // 4, 8, cols), f32),
                 pltpu.SemaphoreType.DMA((24, SWEEPS)),
                 pltpu.SemaphoreType.DMA((24, SWEEPS)),
                 pltpu.SemaphoreType.DMA((nm,)),

time: 42 us -> 38.8 us (0.924)
  Pallas kernels: 38.7 us -> 35.5 us
    pallas_call x1, Pallas kernels: 38.7 us -> 35.5 us  [on_device(): pl.pallas_call(functools.partial(kernel, sizes), out_shape=jax.ShapeDtype...]
where the time goes in v2:
time: 38.8 us; the launch traced here: 38.6 us
  Pallas kernels  35.5 us (91%)
  local copies, waits for them, and re-layouts  3.11 us (8%)
    pallas_call x1, Pallas kernels, on_device(): pl.pallas_call(functools.partial(kernel, sizes), out_shape=jax.ShapeDtype...  35.5 us
    unnamed x1, local copies, waits for them, and re-layouts  3.11 us

profile of v2, /device:TPU:1, one launch (start us, length us, event | category | flops | bytes accessed | tf_op | source)
XLA Modules:
  0.0 38.6 jit_solution(11013496611942152009)
XLA Ops:
  0.0 35.5 %shard_map.28 = f32[16,256,128]{2,1,0:T(8,128)} custom-call(f32[16,256,128]{2,1,0:T(8,128)} %f_hbm.1, f32[16,256,128]{2,1,0:T(8,128)} %s_hbm.1), custom_call_target="tpu_custom_call" | custom-call | tf_op jit(solution)/shard_map/pallas_call | solution.py:479
  35.5 3.1 %copy.4 = f32[16,256,128]{2,1,0:T(8,128)} copy(f32[16,256,128]{2,1,0:T(8,128)} %shard_map.28) | data formatting | bytes 4194304

commit v3 on v2

--- a/solution.py
+++ b/solution.py
@@ -15,7 +15,7 @@
 THIRD = 1.0 / 6.0
 
 
-def kernel(sizes, f_hbm, s_hbm, ov, fv, sv, xb, rb, sr, sb, fb, mh, ml, lz, hz, dg, cn, g, rd, sg, cu, cd, ystage, yland, xystage, xyland, sface, sedge,
+def kernel(sizes, f_hbm, s_hbm, ov, fv, sv, xb, rb, sr, sb, fb, mh, ml, lz, hz, dg, cn, g, rd, sg, cu, cd, dz, ystage, yland, xystage, xyland, sface, sedge,
            send, recv, fsem, ssem):
     ngx, ngy, ngz = sizes
     planes, rows, cols = f_hbm.shape
@@ -64,6 +64,8 @@
     quad = lax.div(lane, 4)
     odd8 = lax.rem(row8 + lane, 2) == 1
     odd_edge = lax.rem(row8 + off, 2) == 0
+    mid = lax.rem(off + 1, 4) >= 2
+    brim = lax.rem(lane + 2, cols) < 4
     first8, last8 = lane == 0, lane == cols - 1
 
     def rep(mask, n):
@@ -230,21 +232,27 @@
             beside = jnp.where(odd_edge, g[2 + m], g[m])
             rd[m] = (((sg[m] + v) + (beside + up)) + ((down + side) + fb[t, m])) * jnp.float32(THIRD)
 
-    def relax(read, i, blk0, n, src, edges, c):
+    def relax(read, i, blk0, n, src, edges, c, inner=False):
         rs = PAD + 8 * blk0
         here = three(read(i, rs, 8 * n))
-        below, above = three(read(i - 1, rs, 8 * n)), three(read(i + 1, rs, 8 * n))
+        below_at, above_at = i - 1, i + 1
+        if inner:
+            below_at, above_at = below_at + (nm - (i - OFF)) // nm, above_at - (i - OFF) // (nm - 1)
+        below, above = three(read(below_at, rs, 8 * n)), three(read(above_at, rs, 8 * n))
         odd = rep(odd8, n)
         beside = jnp.where(odd, above, below) if c == 0 else jnp.where(odd, below, above)
         total = (three(src) + here) + beside
         total = total + three(read(i, rs - 1, 8 * n))
         total = total + three(read(i, rs + 1, 8 * n))
-        edge = jnp.stack(edges, axis=0)
+        return beside_lanes(total, here, edges) * jnp.float32(THIRD)
+
+    def beside_lanes(total, here, edges):
+        n = here.shape[0]
+        edge = jnp.zeros_like(here) if edges is None else jnp.stack(edges, axis=0)
         total = total + jnp.where(rep(first8, n), edge, roll(here, 1))
-        total = total + jnp.where(rep(last8, n), edge, roll(here, -1))
-        return total * jnp.float32(THIRD)
-
-    def red_pair(t, m):
+        return total + jnp.where(rep(last8, n), edge, roll(here, -1))
+
+    def red_pair(t, m, inner=False, edged=True):
         i = m + OFF
 
         def read(i, r, n):
@@ -256,25 +264,68 @@
             return roll(edges_from, -(4 * blk + 2))
 
         for blk0 in range(0, blocks, GROUP):
-            y = relax(read, i, blk0, GROUP, sr[i, pl.ds(PAD + 8 * blk0, 8 * GROUP), :], [edge(blk0 + k) for k in range(GROUP)], 0)
+            edges = [edge(blk0 + k) for k in range(GROUP)] if edged else None
+            y = relax(read, i, blk0, GROUP, sr[i, pl.ds(PAD + 8 * blk0, 8 * GROUP), :], edges, 0, inner)
             rb[i, pl.ds(PAD + 8 * blk0, 8 * GROUP), :] = flat(y)
 
-    def red_rows(t):
-        odd = rep(odd8, nm)
+    def relax_block(x, src, lo, n, r, edges, c):
+        def read(i, r):
+            return x[pl.ds(i, n), pl.ds(r, 8), :]
+
+        odd = rep(odd8, n)
+        here, below, above = read(lo, r), read(lo - 1, r), read(lo + 1, r)
+        total = (src + here) + (jnp.where(odd, above, below) if c == 0 else jnp.where(odd, below, above))
+        total = (total + read(lo, r - 1)) + read(lo, r + 1)
+        return beside_lanes(total, here, edges) * jnp.float32(THIRD)
+
+    def red_rows(t, edged=True):
         for r, e in ((PAD - 8, [roll(cu[m], -2) for m in range(nm)]), (PAD + rows, [roll(cd[m], 2) for m in range(nm)])):
-            def read(i, r):
-                return xb[t, pl.ds(i, nm), pl.ds(r, 8), :]
-
-            here = read(OFF, r)
-            total = (sr[pl.ds(OFF, nm), pl.ds(r, 8), :] + here) + jnp.where(odd, read(OFF + 1, r), read(OFF - 1, r))
-            total = total + read(OFF, r - 1)
-            total = total + read(OFF, r + 1)
-            edge = jnp.stack(e, axis=0)
-            total = total + jnp.where(rep(first8, nm), edge, roll(here, 1))
-            total = total + jnp.where(rep(last8, nm), edge, roll(here, -1))
-            rb[pl.ds(OFF, nm), pl.ds(r, 8), :] = total * jnp.float32(THIRD)
-
-    def black_pair(m, emit):
+            src = sr[pl.ds(OFF, nm), pl.ds(r, 8), :]
+            rb[pl.ds(OFF, nm), pl.ds(r, 8), :] = relax_block(xb.at[t], src, OFF, nm, r, e if edged else None, 0)
+
+    def red_borders(t):
+        for r in (PAD, PAD + rows - 8):
+            src = sr[pl.ds(OFF + 1, nm - 2), pl.ds(r, 8), :]
+            rb[pl.ds(OFF + 1, nm - 2), pl.ds(r, 8), :] = relax_block(xb.at[t], src, OFF + 1, nm - 2, r, None, 0)
+
+    def lift(m, blk):
+        return jnp.where(brim, roll(dz[m], -(4 * blk + 2)), 0.0)
+
+    def black_borders(t):
+        for blk in (0, blocks - 1):
+            r = PAD + 8 * blk
+            y = relax_block(rb, sb[pl.ds(1, nm - 2), pl.ds(8 * blk, 8), :], OFF + 1, nm - 2, r, None, 1)
+            for m in range(1, nm - 1):
+                v = y[m - 1] + lift(m, blk)
+                xb[t + 1, OFF + m, pl.ds(r, 8), :] = v
+                fb[t + 1, m] = jnp.where(quad == blk, roll(v, 4 * blk + 2), fb[t + 1, m] + (dz[m] if blk == 0 else 0.0))
+
+    def edge_response(t):
+        def middle(v):
+            return jnp.where(mid, v, 0.0)
+
+        for m in range(nm):
+            v = middle(g[1 + m])
+            up = pltpu.roll(jnp.where(row8 == 7, jnp.where(lane < 4, middle(cu[m]), roll(v, 4)), v), 1, 0)
+            down = pltpu.roll(jnp.where(row8 == 0, jnp.where(lane >= cols - 4, middle(cd[m]), roll(v, -4)), v), 7, 0)
+            beside = jnp.where(odd_edge, middle(g[2 + m]), middle(g[m]))
+            near = (rd[m] + ((v + beside) + (up + down)) * jnp.float32(THIRD)) * jnp.float32(THIRD)
+            far = jnp.where(off == 0, roll(v, -1), roll(v, 1)) * jnp.float32(THIRD * THIRD)
+            dz[m] = jnp.where(mid, near, far)
+
+    def lift_rest(t):
+        def body(m, carry):
+            v = dz[m]
+            for blk0 in range(0, blocks, GROUP):
+                lo, hi = max(blk0, 1), min(blk0 + GROUP, blocks - 1)
+                rs = pl.ds(PAD + 8 * lo, 8 * (hi - lo))
+                y = jnp.stack([roll(v, -(4 * blk + 2)) for blk in range(lo, hi)], axis=0)
+                xb[t, OFF + m, rs, :] = xb[t, OFF + m, rs, :] + flat(jnp.where(rep(brim, hi - lo), y, 0.0))
+            return carry
+
+        lax.fori_loop(1, nm - 1, body, 0)
+
+    def black_pair(m, emit, edged=True):
         i = m + OFF
 
         def read(i, r, n):
@@ -283,7 +334,7 @@
         edges_from = rd[m]
         for blk0 in range(0, blocks, GROUP):
             rs = pl.ds(8 * blk0, 8 * GROUP)
-            edges = [roll(edges_from, -(4 * (blk0 + k) + 2)) for k in range(GROUP)]
+            edges = [roll(edges_from, -(4 * (blk0 + k) + 2)) for k in range(GROUP)] if edged else None
             emit(blk0, relax(read, i, blk0, GROUP, sb[m, rs, :], edges, 1))
 
     zero = jnp.zeros((rows + 16, cols), jnp.float32)
@@ -418,19 +469,58 @@
         lax.fori_loop(nm - 2, nm, black_body, 0)
 
     def full(t, carry):
-        def emitter(m):
+        def red_inner(m, carry):
+            red_pair(t, m, inner=True, edged=False)
+            return carry
+
+        def black_inner(m, carry):
             parts = [zeros8] * 4
 
             def emit(blk0, y):
                 xb[t + 1, OFF + m, pl.ds(PAD + 8 * blk0, 8 * GROUP), :] = flat(y)
                 pick(parts, y, blk0)
 
-            black_pair(m, emit)
+            black_pair(m, emit, edged=False)
             fb[t + 1, m] = merge(parts)
-
-        sweep(t, emitter)
+            return carry
+
+        lax.fori_loop(0, nm, red_inner, 0)
+        lax.fori_loop(1, nm - 1, black_inner, 0)
+
+        def side(late):
+            arrive_x(t, late)
+            on_first(t, lambda: take_source_x(late))
+            q = at(nm - 1 if late else 0)
+            red_pair(t, q, edged=False)
+            h = int(late)
+
+            @pl.when((flip & has[1 - h]) | (jnp.logical_not(flip) & has[h]))
+            def _():
+                red_pair(t, at(nm if late else -1), edged=False)
+
+            parts = [zeros8] * 4
+
+            def emit(blk0, y):
+                v = y + jnp.stack([lift(q, blk0 + k) for k in range(GROUP)], axis=0)
+                xb[t + 1, OFF + q, pl.ds(PAD + 8 * blk0, 8 * GROUP), :] = flat(v)
+                pick(parts, v, blk0)
+
+            black_pair(q, emit, edged=False)
+            fb[t + 1, q] = merge(parts)
+
+        arrive_faces(t)
+        arrive_diagonals(t)
+        on_first(t, take_source)
+        edge_red(t)
+        edge_response(t)
+        red_rows(t, edged=False)
+        red_borders(t)
+        side(False)
+        side(True)
+        black_borders(t)
         messages(t + 1, lambda m: fb[t + 1, m])
         send_all(t + 1)
+        lift_rest(t + 1)
         return carry
 
     lax.fori_loop(0, SWEEPS - 1, full, 0)
@@ -493,7 +583,7 @@
                 pltpu.VMEM((SWEEPS, 4, 8, cols), f32),
                 pltpu.VMEM((2, SWEEPS, 4, nm // 2, cols), f32),
                 pltpu.VMEM((nm + 2, 8, cols), f32),
-                *[pltpu.VMEM((nm, 8, cols), f32)] * 4,
+                *[pltpu.VMEM((nm, 8, cols), f32)] * 5,
                 *[pltpu.VMEM((2, SWEEPS + 1, nm, 2, cols), f32)] * 2,
                 *[pltpu.VMEM((4, SWEEPS, 1, cols), f32)] * 2,
                 pltpu.VMEM((2, 2, rows // 2, cols), f32),

time: 38.8 us -> 35.6 us (0.918)
  Pallas kernels: 35.5 us -> 32.3 us
    pallas_call x1, Pallas kernels: 35.5 us -> 32.3 us  [on_device(): pl.pallas_call(functools.partial(kernel, sizes), out_shape=jax.ShapeDtype...]
where the time goes in v3:
time: 35.6 us; the launch traced here: 35.5 us
  Pallas kernels  32.3 us (91%)
  local copies, waits for them, and re-layouts  3.11 us (9%)
    pallas_call x1, Pallas kernels, on_device(): pl.pallas_call(functools.partial(kernel, sizes), out_shape=jax.ShapeDtype...  32.3 us
    unnamed x1, local copies, waits for them, and re-layouts  3.11 us

profile of v3, /device:TPU:1, one launch (start us, length us, event | category | flops | bytes accessed | tf_op | source)
XLA Modules:
  0.0 35.5 jit_solution(16652556040386024677)
XLA Ops:
  0.0 32.3 %shard_map.28 = f32[16,256,128]{2,1,0:T(8,128)} custom-call(f32[16,256,128]{2,1,0:T(8,128)} %f_hbm.1, f32[16,256,128]{2,1,0:T(8,128)} %s_hbm.1), custom_call_target="tpu_custom_call" | custom-call | tf_op jit(solution)/shard_map/pallas_call | solution.py:569
  32.3 3.1 %copy.4 = f32[16,256,128]{2,1,0:T(8,128)} copy(f32[16,256,128]{2,1,0:T(8,128)} %shard_map.28) | data formatting | bytes 4194304

commit v4 on v3

--- a/solution.py
+++ b/solution.py
@@ -35,11 +35,6 @@
     def load(ref, to, sem, m):
         return pltpu.make_async_copy(ref.at[pl.ds(2 * m, 2)], to.at[pl.ds(2 * m, 2)], sem.at[m])
 
-    for m in order:
-        load(f_hbm, fv, fsem, m).start()
-    for m in order:
-        load(s_hbm, sv, ssem, m).start()
-
     barrier = pltpu.get_barrier_semaphore()
 
     def greet(device):
@@ -57,6 +52,11 @@
             for d in range(2):
                 greet({"gx": x_to[e], "gy": y_to[d]})
                 greet({"gx": x_to[e], "gz": z_to[d]})
+
+    for m in order:
+        load(f_hbm, fv, fsem, m).start()
+    for m in order:
+        load(s_hbm, sv, ssem, m).start()
 
     row8 = lax.broadcasted_iota(jnp.int32, (8, cols), 0)
     lane = lax.broadcasted_iota(jnp.int32, (8, cols), 1)
@@ -145,7 +145,7 @@
             mh[t, j] = jnp.where(off < 2, even, roll(odd, 2))
             ml[t, j] = jnp.where(off < 2, roll(even, -2), odd)
 
-    def send_all(t):
+    def send_all(t, between=None):
         for e in range(2):
             r = 0 if e == 0 else 7
             for d in range(2):
@@ -156,10 +156,6 @@
                 r = PAD if d == 0 else PAD + rows - 1
                 xystage[2 * e + d, t] = xb[t, OFF + m, pl.ds(r, 1), :]
         for e in range(2):
-            r = PAD if e == 0 else PAD + rows - 2
-            for m in range(nm):
-                ystage[e, t, m] = xb[t, OFF + m, pl.ds(r, 2), :]
-        for e in range(2):
             for d in range(2):
                 yz_copy(t, e, d).start()
         for e in range(2):
@@ -172,7 +168,12 @@
         for e in range(2):
             z_copy(t, e).start()
         for e in range(2):
+            r = PAD if e == 0 else PAD + rows - 2
+            for m in range(nm):
+                ystage[e, t, m] = xb[t, OFF + m, pl.ds(r, 2), :]
             y_copy(t, e).start()
+        if between is not None:
+            between()
         for e in range(2):
             @pl.when(has[e])
             def _():
@@ -209,13 +210,19 @@
             def _():
                 for d in range(2):
                     xz_copy(t, 1 - e, d, e).wait_recv()
+                k = -1 if e == 0 else 1
+                g[0 if e == 0 else nm + 1] = jnp.where(off == 2, roll(dg[t, 2 * e], k), roll(dg[t, 2 * e + 1], k))
+
+    def arrive_xy(t):
+        for e in range(2):
+            @pl.when(has[e])
+            def _():
+                for d in range(2):
                     xy_copy(t, 1 - e, d, e).wait_recv()
                 i = OFF - 1 if e == 0 else OFF + nm
                 for d in range(2):
                     r = PAD - 1 if d == 0 else PAD + rows
                     xb[t, i, pl.ds(r, 1), :] = xyland[2 * e + d, t]
-                k = -1 if e == 0 else 1
-                g[0 if e == 0 else nm + 1] = jnp.where(off == 2, roll(dg[t, 2 * e], k), roll(dg[t, 2 * e + 1], k))
 
     def arrive_x(t, late):
         for e in range(2):
@@ -232,7 +239,7 @@
             beside = jnp.where(odd_edge, g[2 + m], g[m])
             rd[m] = (((sg[m] + v) + (beside + up)) + ((down + side) + fb[t, m])) * jnp.float32(THIRD)
 
-    def relax(read, i, blk0, n, src, edges, c, inner=False):
+    def relax(read, i, blk0, n, src, c, inner=False):
         rs = PAD + 8 * blk0
         here = three(read(i, rs, 8 * n))
         below_at, above_at = i - 1, i + 1
@@ -244,49 +251,48 @@
         total = (three(src) + here) + beside
         total = total + three(read(i, rs - 1, 8 * n))
         total = total + three(read(i, rs + 1, 8 * n))
-        return beside_lanes(total, here, edges) * jnp.float32(THIRD)
-
-    def beside_lanes(total, here, edges):
+        return beside_lanes(total, here) * jnp.float32(THIRD)
+
+    def beside_lanes(total, here):
         n = here.shape[0]
-        edge = jnp.zeros_like(here) if edges is None else jnp.stack(edges, axis=0)
-        total = total + jnp.where(rep(first8, n), edge, roll(here, 1))
-        return total + jnp.where(rep(last8, n), edge, roll(here, -1))
-
-    def red_pair(t, m, inner=False, edged=True):
+        total = total + jnp.where(rep(first8, n), 0.0, roll(here, 1))
+        return total + jnp.where(rep(last8, n), 0.0, roll(here, -1))
+
+    def red_pair(t, m, inner=False, keep=None):
         i = m + OFF
 
         def read(i, r, n):
             return xb[t, i, pl.ds(r, n), :]
 
-        edges_from = g[m + 1]
-
-        def edge(blk):
-            return roll(edges_from, -(4 * blk + 2))
-
         for blk0 in range(0, blocks, GROUP):
-            edges = [edge(blk0 + k) for k in range(GROUP)] if edged else None
-            y = relax(read, i, blk0, GROUP, sr[i, pl.ds(PAD + 8 * blk0, 8 * GROUP), :], edges, 0, inner)
+            y = relax(read, i, blk0, GROUP, sr[i, pl.ds(PAD + 8 * blk0, 8 * GROUP), :], 0, inner)
+            if keep is not None:
+                y = jnp.where(keep, y, 0.0)
             rb[i, pl.ds(PAD + 8 * blk0, 8 * GROUP), :] = flat(y)
 
-    def relax_block(x, src, lo, n, r, edges, c):
+    def relax_block(x, src, lo, n, r, c, inner=False):
         def read(i, r):
             return x[pl.ds(i, n), pl.ds(r, 8), :]
 
         odd = rep(odd8, n)
-        here, below, above = read(lo, r), read(lo - 1, r), read(lo + 1, r)
+        here = read(lo, r)
+        if inner:
+            below, above = (jnp.concatenate(p, axis=0) for p in ((here[:1], here[:-1]), (here[1:], here[-1:])))
+        else:
+            below, above = read(lo - 1, r), read(lo + 1, r)
         total = (src + here) + (jnp.where(odd, above, below) if c == 0 else jnp.where(odd, below, above))
         total = (total + read(lo, r - 1)) + read(lo, r + 1)
-        return beside_lanes(total, here, edges) * jnp.float32(THIRD)
-
-    def red_rows(t, edged=True):
-        for r, e in ((PAD - 8, [roll(cu[m], -2) for m in range(nm)]), (PAD + rows, [roll(cd[m], 2) for m in range(nm)])):
+        return beside_lanes(total, here) * jnp.float32(THIRD)
+
+    def red_rows(t):
+        for r in (PAD - 8, PAD + rows):
             src = sr[pl.ds(OFF, nm), pl.ds(r, 8), :]
-            rb[pl.ds(OFF, nm), pl.ds(r, 8), :] = relax_block(xb.at[t], src, OFF, nm, r, e if edged else None, 0)
+            rb[pl.ds(OFF, nm), pl.ds(r, 8), :] = relax_block(xb.at[t], src, OFF, nm, r, 0)
 
     def red_borders(t):
         for r in (PAD, PAD + rows - 8):
-            src = sr[pl.ds(OFF + 1, nm - 2), pl.ds(r, 8), :]
-            rb[pl.ds(OFF + 1, nm - 2), pl.ds(r, 8), :] = relax_block(xb.at[t], src, OFF + 1, nm - 2, r, None, 0)
+            src = sr[pl.ds(OFF, nm), pl.ds(r, 8), :]
+            rb[pl.ds(OFF, nm), pl.ds(r, 8), :] = relax_block(xb.at[t], src, OFF, nm, r, 0, inner=True)
 
     def lift(m, blk):
         return jnp.where(brim, roll(dz[m], -(4 * blk + 2)), 0.0)
@@ -294,11 +300,17 @@
     def black_borders(t):
         for blk in (0, blocks - 1):
             r = PAD + 8 * blk
-            y = relax_block(rb, sb[pl.ds(1, nm - 2), pl.ds(8 * blk, 8), :], OFF + 1, nm - 2, r, None, 1)
+            y = relax_block(rb, sb[pl.ds(1, nm - 2), pl.ds(8 * blk, 8), :], OFF + 1, nm - 2, r, 1)
+            xb[t + 1, pl.ds(OFF + 1, nm - 2), pl.ds(r, 8), :] = y
             for m in range(1, nm - 1):
-                v = y[m - 1] + lift(m, blk)
-                xb[t + 1, OFF + m, pl.ds(r, 8), :] = v
-                fb[t + 1, m] = jnp.where(quad == blk, roll(v, 4 * blk + 2), fb[t + 1, m] + (dz[m] if blk == 0 else 0.0))
+                fb[t + 1, m] = jnp.where(quad == blk, roll(y[m - 1], 4 * blk + 2), fb[t + 1, m])
+
+    def lift_borders(t):
+        for m in range(1, nm - 1):
+            for blk in (0, blocks - 1):
+                rs = pl.ds(PAD + 8 * blk, 8)
+                xb[t, OFF + m, rs, :] = xb[t, OFF + m, rs, :] + lift(m, blk)
+            fb[t, m] = fb[t, m] + dz[m]
 
     def edge_response(t):
         def middle(v):
@@ -313,29 +325,30 @@
             far = jnp.where(off == 0, roll(v, -1), roll(v, 1)) * jnp.float32(THIRD * THIRD)
             dz[m] = jnp.where(mid, near, far)
 
+    def lift_pair(t, m, first, last):
+        v = dz[m]
+        for blk0 in range(0, blocks, GROUP):
+            lo, hi = max(blk0, first), min(blk0 + GROUP, last)
+            rs = pl.ds(PAD + 8 * lo, 8 * (hi - lo))
+            y = jnp.stack([roll(v, -(4 * blk + 2)) for blk in range(lo, hi)], axis=0)
+            xb[t, OFF + m, rs, :] = xb[t, OFF + m, rs, :] + flat(jnp.where(rep(brim, hi - lo), y, 0.0))
+
     def lift_rest(t):
         def body(m, carry):
-            v = dz[m]
-            for blk0 in range(0, blocks, GROUP):
-                lo, hi = max(blk0, 1), min(blk0 + GROUP, blocks - 1)
-                rs = pl.ds(PAD + 8 * lo, 8 * (hi - lo))
-                y = jnp.stack([roll(v, -(4 * blk + 2)) for blk in range(lo, hi)], axis=0)
-                xb[t, OFF + m, rs, :] = xb[t, OFF + m, rs, :] + flat(jnp.where(rep(brim, hi - lo), y, 0.0))
+            lift_pair(t, m, 1, blocks - 1)
             return carry
 
         lax.fori_loop(1, nm - 1, body, 0)
 
-    def black_pair(m, emit, edged=True):
+    def black_pair(m, emit):
         i = m + OFF
 
         def read(i, r, n):
             return rb[i, pl.ds(r, n), :]
 
-        edges_from = rd[m]
         for blk0 in range(0, blocks, GROUP):
             rs = pl.ds(8 * blk0, 8 * GROUP)
-            edges = [roll(edges_from, -(4 * (blk0 + k) + 2)) for k in range(GROUP)] if edged else None
-            emit(blk0, relax(read, i, blk0, GROUP, sb[m, rs, :], edges, 1))
+            emit(blk0, relax(read, i, blk0, GROUP, sb[m, rs, :], 1))
 
     zero = jnp.zeros((rows + 16, cols), jnp.float32)
     for e in range(2):
@@ -375,8 +388,6 @@
 
     lax.fori_loop(0, nm // 2, pack_field, 0)
     messages(0, lambda m: fb[0, m])
-    pl.semaphore_wait(barrier, 8 + 5 * (has_lo.astype(jnp.int32) + has_hi.astype(jnp.int32)))
-    send_all(0)
     lax.fori_loop(0, nm // 2, pack_source, 0)
     half = rows // 2
     odd_lane = lax.rem(lax.broadcasted_iota(jnp.int32, (half, cols), 1), 2) == 1
@@ -384,12 +395,17 @@
         for j in range(nm // 4):
             parts = [roll(sg[4 * j + k], k - 2 + e) for k in range(4)]
             sedge[0, e, j] = jnp.where(off < 2, jnp.where(off == 0, parts[0], parts[1]), jnp.where(off == 2, parts[2], parts[3]))
-        sz_copy(e).start()
-    for e in range(2):
         r = PAD if e == 0 else PAD + rows - 1
         for m in range(nm):
             ystage[e, SWEEPS, m, pl.ds(0, 1), :] = sr[OFF + m, pl.ds(r, 1), :]
-        sy_copy(e).start()
+
+    pl.semaphore_wait(barrier, 8 + 5 * (has_lo.astype(jnp.int32) + has_hi.astype(jnp.int32)))
+    def send_source():
+        for e in range(2):
+            sz_copy(e).start()
+            sy_copy(e).start()
+
+    send_all(0, send_source)
     for e in range(2):
         @pl.when(has[e])
         def _():
@@ -425,52 +441,12 @@
     def at(p):
         return jnp.where(flip, nm - 1 - p, p)
 
-    def half_red(t, p):
-        red_pair(t, at(p))
-
-    def halo_red(t, late):
-        late = int(late)
-
-        @pl.when((flip & has[1 - late]) | (jnp.logical_not(flip) & has[late]))
-        def _():
-            red_pair(t, at(nm if late else -1))
-
     def on_first(t, do):
-        if not isinstance(t, int):
-            pl.when(t == 0)(do)
-        elif t == 0:
-            do()
-
-    def sweep(t, emitter):
-        arrive_faces(t)
-        arrive_x(t, False)
-
-        def red_body(p, carry):
-            half_red(t, p)
-            return carry
-
-        lax.fori_loop(0, nm - 1, red_body, 0)
-        arrive_diagonals(t)
-        on_first(t, take_source)
-        edge_red(t)
-        red_rows(t)
-        on_first(t, lambda: take_source_x(False))
-        halo_red(t, False)
-
-        def black_body(p, carry):
-            emitter(at(p))
-            return carry
-
-        lax.fori_loop(0, nm - 2, black_body, 0)
-        arrive_x(t, True)
-        lax.fori_loop(nm - 1, nm, red_body, 0)
-        on_first(t, lambda: take_source_x(True))
-        halo_red(t, True)
-        lax.fori_loop(nm - 2, nm, black_body, 0)
+        pl.when(t == 0)(do)
 
     def full(t, carry):
         def red_inner(m, carry):
-            red_pair(t, m, inner=True, edged=False)
+            red_pair(t, m, inner=True)
             return carry
 
         def black_inner(m, carry):
@@ -480,62 +456,82 @@
                 xb[t + 1, OFF + m, pl.ds(PAD + 8 * blk0, 8 * GROUP), :] = flat(y)
                 pick(parts, y, blk0)
 
-            black_pair(m, emit, edged=False)
+            black_pair(m, emit)
             fb[t + 1, m] = merge(parts)
             return carry
 
         lax.fori_loop(0, nm, red_inner, 0)
         lax.fori_loop(1, nm - 1, black_inner, 0)
 
-        def side(late):
+        def side_red(late):
             arrive_x(t, late)
             on_first(t, lambda: take_source_x(late))
+            h = int(late)
+            keep = jnp.where(flip, has[1 - h], has[h])
+            red_pair(t, at(nm - 1 if late else 0))
+            red_pair(t, at(nm if late else -1), keep=keep)
+
+        def side_black(late):
             q = at(nm - 1 if late else 0)
-            red_pair(t, q, edged=False)
-            h = int(late)
-
-            @pl.when((flip & has[1 - h]) | (jnp.logical_not(flip) & has[h]))
-            def _():
-                red_pair(t, at(nm if late else -1), edged=False)
-
             parts = [zeros8] * 4
 
             def emit(blk0, y):
-                v = y + jnp.stack([lift(q, blk0 + k) for k in range(GROUP)], axis=0)
-                xb[t + 1, OFF + q, pl.ds(PAD + 8 * blk0, 8 * GROUP), :] = flat(v)
-                pick(parts, v, blk0)
-
-            black_pair(q, emit, edged=False)
+                if late:
+                    y = y + jnp.stack([lift(q, blk0 + k) for k in range(GROUP)], axis=0)
+                xb[t + 1, OFF + q, pl.ds(PAD + 8 * blk0, 8 * GROUP), :] = flat(y)
+                pick(parts, y, blk0)
+
+            black_pair(q, emit)
             fb[t + 1, q] = merge(parts)
 
         arrive_faces(t)
+        arrive_xy(t)
+        red_borders(t)
+        side_red(False)
+        on_first(t, take_source)
+        red_rows(t)
+        black_borders(t)
+        side_black(False)
         arrive_diagonals(t)
-        on_first(t, take_source)
         edge_red(t)
         edge_response(t)
-        red_rows(t, edged=False)
-        red_borders(t)
-        side(False)
-        side(True)
-        black_borders(t)
-        messages(t + 1, lambda m: fb[t + 1, m])
-        send_all(t + 1)
-        lift_rest(t + 1)
+        lift_borders(t + 1)
+        early = at(0)
+        lift_pair(t + 1, early, 0, blocks)
+        fb[t + 1, early] = fb[t + 1, early] + dz[early]
+        side_red(True)
+        side_black(True)
+
+        @pl.when(t < SWEEPS - 1)
+        def _():
+            messages(t + 1, lambda m: fb[t + 1, m])
+            send_all(t + 1)
+            lift_rest(t + 1)
+
         return carry
 
-    lax.fori_loop(0, SWEEPS - 1, full, 0)
-
-    def final(m):
-        def emit(blk0, y):
-            red = three(rb[OFF + m, pl.ds(PAD + 8 * blk0, 8 * GROUP), :])
-            rs = pl.ds(8 * blk0, 8 * GROUP)
-            odd = rep(odd8, GROUP)
-            ov[2 * m, rs, :] = flat(jnp.where(odd, y, red))
-            ov[2 * m + 1, rs, :] = flat(jnp.where(odd, red, y))
-
-        black_pair(m, emit)
-
-    sweep(SWEEPS - 1, final)
+    lax.fori_loop(0, SWEEPS, full, 0)
+    for m in (0, nm - 1):
+        dz[m] = zeros8
+
+    def write(m, carry):
+        lr = jnp.where(mid, g[1 + m], 0.0) * jnp.float32(THIRD)
+        lb = dz[m]
+        low, high = jnp.where(odd_edge, lr, lb), jnp.where(odd_edge, lb, lr)
+        low_red, high_red = jnp.where(odd_edge, lr, 0.0), jnp.where(odd_edge, 0.0, lr)
+        for blk0 in range(0, blocks, GROUP):
+            rs, ps = pl.ds(8 * blk0, 8 * GROUP), pl.ds(PAD + 8 * blk0, 8 * GROUP)
+            red, black = three(rb[OFF + m, ps, :]), three(xb[SWEEPS, OFF + m, ps, :])
+            odd, edge = rep(odd8, GROUP), rep(brim, GROUP)
+
+            def add(inside, outer):
+                return jnp.stack([roll(outer if blk in (0, blocks - 1) else inside, -(4 * blk + 2)) for blk in range(blk0, blk0 + GROUP)], axis=0)
+
+            ov[2 * m, rs, :] = flat(jnp.where(odd, black, red) + jnp.where(edge, add(low, low_red), 0.0))
+            ov[2 * m + 1, rs, :] = flat(jnp.where(odd, red, black) + jnp.where(edge, add(high, high_red), 0.0))
+        return carry
+
+    lax.fori_loop(0, nm, write, 0, unroll=2)
 
     def drain(t, carry):
         for c in face_copies(t):
@@ -574,11 +570,11 @@
             scratch_shapes=[
                 pltpu.VMEM(field.shape, f32),
                 pltpu.VMEM(field.shape, f32),
-                pltpu.VMEM((SWEEPS, *wide), f32),
+                pltpu.VMEM((SWEEPS + 1, *wide), f32),
                 pltpu.VMEM(wide, f32),
                 pltpu.VMEM(wide, f32),
                 pltpu.VMEM((nm, rows, cols), f32),
-                pltpu.VMEM((SWEEPS, nm, 8, cols), f32),
+                pltpu.VMEM((SWEEPS + 1, nm, 8, cols), f32),
                 *[pltpu.VMEM((SWEEPS, nm // 2, 8, cols), f32)] * 4,
                 pltpu.VMEM((SWEEPS, 4, 8, cols), f32),
                 pltpu.VMEM((2, SWEEPS, 4, nm // 2, cols), f32),

time: 35.6 us -> 34.7 us (0.975)
  Pallas kernels: 32.3 us -> 31.5 us
    pallas_call x1, Pallas kernels: 32.3 us -> 31.5 us  [on_device(): pl.pallas_call(functools.partial(kernel, sizes), out_shape=jax.ShapeDtype...]
where the time goes in v4:
time: 34.7 us; the launch traced here: 34.6 us
  Pallas kernels  31.5 us (91%)
  local copies, waits for them, and re-layouts  3.11 us (9%)
    pallas_call x1, Pallas kernels, on_device(): pl.pallas_call(functools.partial(kernel, sizes), out_shape=jax.ShapeDtype...  31.5 us
    unnamed x1, local copies, waits for them, and re-layouts  3.11 us

profile of v4, /device:TPU:1, one launch (start us, length us, event | category | flops | bytes accessed | tf_op | source)
XLA Modules:
  0.0 34.6 jit_solution(10519892064635194785)
XLA Ops:
  0.0 31.5 %shard_map.28 = f32[16,256,128]{2,1,0:T(8,128)} custom-call(f32[16,256,128]{2,1,0:T(8,128)} %f_hbm.1, f32[16,256,128]{2,1,0:T(8,128)} %s_hbm.1), custom_call_target="tpu_custom_call" | custom-call | tf_op jit(solution)/shard_map/pallas_call | solution.py:565
  31.5 3.1 %copy.4 = f32[16,256,128]{2,1,0:T(8,128)} copy(f32[16,256,128]{2,1,0:T(8,128)} %shard_map.28) | data formatting | bytes 4194304

commit v5 on v4

--- a/solution.py
+++ b/solution.py
@@ -62,7 +62,8 @@
     lane = lax.broadcasted_iota(jnp.int32, (8, cols), 1)
     off = lax.rem(lane, 4)
     quad = lax.div(lane, 4)
-    odd8 = lax.rem(row8 + lane, 2) == 1
+    parity8 = lax.rem(row8 + lane, 2)
+    odd8 = parity8 == 1
     odd_edge = lax.rem(row8 + off, 2) == 0
     mid = lax.rem(off + 1, 4) >= 2
     brim = lax.rem(lane + 2, cols) < 4
@@ -179,15 +180,17 @@
             def _():
                 x_copy(t, e).start()
 
-    def arrive_faces(t):
-        for e in range(2):
-            z_copy(t, e).wait_recv()
+    def arrive_y(t):
         for e in range(2):
             y_copy(t, e).wait_recv()
         for e in range(2):
             r = PAD - 2 if e == 0 else PAD + rows
             for m in range(nm):
                 xb[t, OFF + m, pl.ds(r, 2), :] = yland[e, t, m]
+
+    def arrive_z(t):
+        for e in range(2):
+            z_copy(t, e).wait_recv()
         for j in range(nm // 2):
             low, high = lz[t, j], hz[t, j]
             l1, l3, lm = roll(low, 1), roll(low, 3), roll(low, -1)
@@ -205,6 +208,7 @@
                 cu[2 * j + p] = jnp.where(off == 2, roll(a, 5 - 2 * p), roll(b, 5 - 2 * p))
                 a, b = (jnp.broadcast_to(cn[0, t, k, pl.ds(j, 1), :], (8, cols)) for k in (2, 3))
                 cd[2 * j + p] = jnp.where(off == 2, roll(a, -3 - 2 * p), roll(b, -3 - 2 * p))
+    def arrive_xz(t):
         for e in range(2):
             @pl.when(has[e])
             def _():
@@ -244,7 +248,7 @@
         here = three(read(i, rs, 8 * n))
         below_at, above_at = i - 1, i + 1
         if inner:
-            below_at, above_at = below_at + (nm - (i - OFF)) // nm, above_at - (i - OFF) // (nm - 1)
+            below_at, above_at = below_at - (nm - (i - OFF)) // nm, above_at - (OFF + nm) * ((i - OFF) // (nm - 1))
         below, above = three(read(below_at, rs, 8 * n)), three(read(above_at, rs, 8 * n))
         odd = rep(odd8, n)
         beside = jnp.where(odd, above, below) if c == 0 else jnp.where(odd, below, above)
@@ -270,16 +274,12 @@
                 y = jnp.where(keep, y, 0.0)
             rb[i, pl.ds(PAD + 8 * blk0, 8 * GROUP), :] = flat(y)
 
-    def relax_block(x, src, lo, n, r, c, inner=False):
+    def relax_block(x, src, lo, n, r, c):
         def read(i, r):
             return x[pl.ds(i, n), pl.ds(r, 8), :]
 
         odd = rep(odd8, n)
-        here = read(lo, r)
-        if inner:
-            below, above = (jnp.concatenate(p, axis=0) for p in ((here[:1], here[:-1]), (here[1:], here[-1:])))
-        else:
-            below, above = read(lo - 1, r), read(lo + 1, r)
+        here, below, above = read(lo, r), read(lo - 1, r), read(lo + 1, r)
         total = (src + here) + (jnp.where(odd, above, below) if c == 0 else jnp.where(odd, below, above))
         total = (total + read(lo, r - 1)) + read(lo, r + 1)
         return beside_lanes(total, here) * jnp.float32(THIRD)
@@ -290,9 +290,17 @@
             rb[pl.ds(OFF, nm), pl.ds(r, 8), :] = relax_block(xb.at[t], src, OFF, nm, r, 0)
 
     def red_borders(t):
-        for r in (PAD, PAD + rows - 8):
-            src = sr[pl.ds(OFF, nm), pl.ds(r, 8), :]
-            rb[pl.ds(OFF, nm), pl.ds(r, 8), :] = relax_block(xb.at[t], src, OFF, nm, r, 0, inner=True)
+        for r, d, k in ((PAD, -1, 0), (PAD + rows - 8, 1, 7)):
+            halo = xb[t, pl.ds(OFF, nm), pl.ds(r + d, 8), :]
+            own = pl.ds(OFF, nm), pl.ds(r, 8), slice(None)
+            rb[own] = rb[own] + jnp.where(jnp.broadcast_to((row8 == k)[None], (nm, 8, cols)), halo, 0.0) * jnp.float32(THIRD)
+
+    def red_side(t, q, h, low):
+        near = parity8 == jnp.where(low, 0, 1)
+        for blk0 in range(0, blocks, GROUP):
+            rs = pl.ds(PAD + 8 * blk0, 8 * GROUP)
+            halo = jnp.where(rep(near, GROUP), three(xb[t, h + OFF, rs, :]), 0.0)
+            rb[q + OFF, rs, :] = rb[q + OFF, rs, :] + flat(halo * jnp.float32(THIRD))
 
     def lift(m, blk):
         return jnp.where(brim, roll(dz[m], -(4 * blk + 2)), 0.0)
@@ -415,6 +423,11 @@
             sface[0, e] = jnp.where(odd_lane, odd, even) if e == 0 else jnp.where(odd_lane, even, odd)
             sx_copy(e).start()
 
+    for t in range(SWEEPS):
+        xb[t, 0, pl.ds(PAD, rows), :] = zero[:rows]
+        for r in (PAD - 8, PAD + rows):
+            xb[t, pl.ds(OFF, nm), pl.ds(r, 8), :] = jnp.zeros((nm, 8, cols), jnp.float32)
+
     def take_source():
         for e in range(2):
             sz_copy(e).wait_recv()
@@ -464,12 +477,11 @@
         lax.fori_loop(1, nm - 1, black_inner, 0)
 
         def side_red(late):
-            arrive_x(t, late)
-            on_first(t, lambda: take_source_x(late))
             h = int(late)
-            keep = jnp.where(flip, has[1 - h], has[h])
-            red_pair(t, at(nm - 1 if late else 0))
-            red_pair(t, at(nm if late else -1), keep=keep)
+            q = at(nm - 1 if late else 0)
+            out = at(nm if late else -1)
+            red_side(t, q, out, flip if late else jnp.logical_not(flip))
+            red_pair(t, out, keep=jnp.where(flip, has[1 - h], has[h]))
 
         def side_black(late):
             q = at(nm - 1 if late else 0)
@@ -484,14 +496,18 @@
             black_pair(q, emit)
             fb[t + 1, q] = merge(parts)
 
-        arrive_faces(t)
+        arrive_y(t)
+        red_borders(t)
+        arrive_x(t, False)
+        on_first(t, lambda: take_source_x(False))
         arrive_xy(t)
-        red_borders(t)
         side_red(False)
         on_first(t, take_source)
         red_rows(t)
         black_borders(t)
         side_black(False)
+        arrive_xz(t)
+        arrive_z(t)
         arrive_diagonals(t)
         edge_red(t)
         edge_response(t)
@@ -499,6 +515,8 @@
         early = at(0)
         lift_pair(t + 1, early, 0, blocks)
         fb[t + 1, early] = fb[t + 1, early] + dz[early]
+        arrive_x(t, True)
+        on_first(t, lambda: take_source_x(True))
         side_red(True)
         side_black(True)
 

time: 34.7 us -> 33.9 us (0.977)
  Pallas kernels: 31.5 us -> 30.7 us
    pallas_call x1, Pallas kernels: 31.5 us -> 30.7 us  [on_device(): pl.pallas_call(functools.partial(kernel, sizes), out_shape=jax.ShapeDtype...]
where the time goes in v5:
time: 33.9 us; the launch traced here: 33.8 us
  Pallas kernels  30.7 us (91%)
  local copies, waits for them, and re-layouts  3.11 us (9%)
    pallas_call x1, Pallas kernels, on_device(): pl.pallas_call(functools.partial(kernel, sizes), out_shape=jax.ShapeDtype...  30.7 us
    unnamed x1, local copies, waits for them, and re-layouts  3.11 us

profile of v5, /device:TPU:1, one launch (start us, length us, event | category | flops | bytes accessed | tf_op | source)
XLA Modules:
  0.0 33.8 jit_solution(17532875200620075409)
XLA Ops:
  0.0 30.7 %shard_map.28 = f32[16,256,128]{2,1,0:T(8,128)} custom-call(f32[16,256,128]{2,1,0:T(8,128)} %f_hbm.1, f32[16,256,128]{2,1,0:T(8,128)} %s_hbm.1), custom_call_target="tpu_custom_call" | custom-call | tf_op jit(solution)/shard_map/pallas_call | solution.py:583
  30.7 3.1 %copy.4 = f32[16,256,128]{2,1,0:T(8,128)} copy(f32[16,256,128]{2,1,0:T(8,128)} %shard_map.28) | data formatting | bytes 4194304

commit v6 on v5

--- a/solution.py
+++ b/solution.py
@@ -289,11 +289,11 @@
             src = sr[pl.ds(OFF, nm), pl.ds(r, 8), :]
             rb[pl.ds(OFF, nm), pl.ds(r, 8), :] = relax_block(xb.at[t], src, OFF, nm, r, 0)
 
-    def red_borders(t):
+    def red_borders(t, i, n):
         for r, d, k in ((PAD, -1, 0), (PAD + rows - 8, 1, 7)):
-            halo = xb[t, pl.ds(OFF, nm), pl.ds(r + d, 8), :]
-            own = pl.ds(OFF, nm), pl.ds(r, 8), slice(None)
-            rb[own] = rb[own] + jnp.where(jnp.broadcast_to((row8 == k)[None], (nm, 8, cols)), halo, 0.0) * jnp.float32(THIRD)
+            halo = xb[t, pl.ds(i, n), pl.ds(r + d, 8), :]
+            own = pl.ds(i, n), pl.ds(r, 8), slice(None)
+            rb[own] = rb[own] + jnp.where(jnp.broadcast_to((row8 == k)[None], (n, 8, cols)), halo, 0.0) * jnp.float32(THIRD)
 
     def red_side(t, q, h, low):
         near = parity8 == jnp.where(low, 0, 1)
@@ -308,10 +308,10 @@
     def black_borders(t):
         for blk in (0, blocks - 1):
             r = PAD + 8 * blk
-            y = relax_block(rb, sb[pl.ds(1, nm - 2), pl.ds(8 * blk, 8), :], OFF + 1, nm - 2, r, 1)
-            xb[t + 1, pl.ds(OFF + 1, nm - 2), pl.ds(r, 8), :] = y
-            for m in range(1, nm - 1):
-                fb[t + 1, m] = jnp.where(quad == blk, roll(y[m - 1], 4 * blk + 2), fb[t + 1, m])
+            y = relax_block(rb, sb[:, pl.ds(8 * blk, 8), :], OFF, nm, r, 1)
+            xb[t + 1, pl.ds(OFF, nm), pl.ds(r, 8), :] = y
+            for m in range(nm):
+                fb[t + 1, m] = jnp.where(quad == blk, roll(y[m], 4 * blk + 2), fb[t + 1, m])
 
     def lift_borders(t):
         for m in range(1, nm - 1):
@@ -426,7 +426,7 @@
     for t in range(SWEEPS):
         xb[t, 0, pl.ds(PAD, rows), :] = zero[:rows]
         for r in (PAD - 8, PAD + rows):
-            xb[t, pl.ds(OFF, nm), pl.ds(r, 8), :] = jnp.zeros((nm, 8, cols), jnp.float32)
+            xb[t, pl.ds(OFF - 1, nm + 2), pl.ds(r, 8), :] = jnp.zeros((nm + 2, 8, cols), jnp.float32)
 
     def take_source():
         for e in range(2):
@@ -496,16 +496,17 @@
             black_pair(q, emit)
             fb[t + 1, q] = merge(parts)
 
-        arrive_y(t)
-        red_borders(t)
         arrive_x(t, False)
         on_first(t, lambda: take_source_x(False))
+        side_red(False)
+        side_black(False)
+        arrive_y(t)
+        red_borders(t, OFF, nm)
         arrive_xy(t)
-        side_red(False)
+        red_borders(t, at(-1) + OFF, 1)
         on_first(t, take_source)
         red_rows(t)
         black_borders(t)
-        side_black(False)
         arrive_xz(t)
         arrive_z(t)
         arrive_diagonals(t)

time: 33.9 us -> 33.5 us (0.988)
  Pallas kernels: 30.7 us -> 30.3 us
    pallas_call x1, Pallas kernels: 30.7 us -> 30.3 us  [on_device(): pl.pallas_call(functools.partial(kernel, sizes), out_shape=jax.ShapeDtype...]
where the time goes in v6:
time: 33.5 us; the launch traced here: 33.4 us
  Pallas kernels  30.3 us (90%)
  local copies, waits for them, and re-layouts  3.11 us (9%)
    pallas_call x1, Pallas kernels, on_device(): pl.pallas_call(functools.partial(kernel, sizes), out_shape=jax.ShapeDtype...  30.3 us
    unnamed x1, local copies, waits for them, and re-layouts  3.11 us

profile of v6, /device:TPU:1, one launch (start us, length us, event | category | flops | bytes accessed | tf_op | source)
XLA Modules:
  0.0 33.4 jit_solution(11232050830056915084)
XLA Ops:
  0.0 30.3 %shard_map.28 = f32[16,256,128]{2,1,0:T(8,128)} custom-call(f32[16,256,128]{2,1,0:T(8,128)} %f_hbm.1, f32[16,256,128]{2,1,0:T(8,128)} %s_hbm.1), custom_call_target="tpu_custom_call" | custom-call | tf_op jit(solution)/shard_map/pallas_call | solution.py:584
  30.3 3.1 %copy.4 = f32[16,256,128]{2,1,0:T(8,128)} copy(f32[16,256,128]{2,1,0:T(8,128)} %shard_map.28) | data formatting | bytes 4194304

commit v7 on v6

--- a/solution.py
+++ b/solution.py
@@ -457,6 +457,24 @@
     def on_first(t, do):
         pl.when(t == 0)(do)
 
+    def drain(t):
+        for c in face_copies(t):
+            c.wait_send()
+        for e in range(2):
+            @pl.when(has[e])
+            def _():
+                for c in wall_copies(t, e):
+                    c.wait_send()
+
+    def drain_source():
+        for e in range(2):
+            sz_copy(e).wait_send()
+            sy_copy(e).wait_send()
+
+            @pl.when(has[e])
+            def _():
+                sx_copy(e).wait_send()
+
     def full(t, carry):
         def red_inner(m, carry):
             red_pair(t, m, inner=True)
@@ -475,6 +493,8 @@
 
         lax.fori_loop(0, nm, red_inner, 0)
         lax.fori_loop(1, nm - 1, black_inner, 0)
+        drain(t)
+        pl.when(t == 1)(drain_source)
 
         def side_red(late):
             h = int(late)
@@ -550,26 +570,7 @@
             ov[2 * m + 1, rs, :] = flat(jnp.where(odd, red, black) + jnp.where(edge, add(high, high_red), 0.0))
         return carry
 
-    lax.fori_loop(0, nm, write, 0, unroll=2)
-
-    def drain(t, carry):
-        for c in face_copies(t):
-            c.wait_send()
-        for e in range(2):
-            @pl.when(has[e])
-            def _():
-                for c in wall_copies(t, e):
-                    c.wait_send()
-        return carry
-
-    lax.fori_loop(0, SWEEPS, drain, 0)
-    for e in range(2):
-        sz_copy(e).wait_send()
-        sy_copy(e).wait_send()
-
-        @pl.when(has[e])
-        def _():
-            sx_copy(e).wait_send()
+    lax.fori_loop(0, nm, write, 0, unroll=4)
 
 
 def solution(mesh):

time: 33.5 us -> 33.3 us (level)
  no operation moved by 1% of the time
where the time goes in v7:
time: 33.3 us; the launch traced here: 33.2 us
  Pallas kernels  30 us (90%)
  local copies, waits for them, and re-layouts  3.11 us (9%)
    pallas_call x1, Pallas kernels, on_device(): pl.pallas_call(functools.partial(kernel, sizes), out_shape=jax.ShapeDtype...  30 us
    unnamed x1, local copies, waits for them, and re-layouts  3.11 us

profile of v7, /device:TPU:1, one launch (start us, length us, event | category | flops | bytes accessed | tf_op | source)
XLA Modules:
  0.0 33.2 jit_solution(588044120239927164)
XLA Ops:
  0.0 30.0 %shard_map.28 = f32[16,256,128]{2,1,0:T(8,128)} custom-call(f32[16,256,128]{2,1,0:T(8,128)} %f_hbm.1, f32[16,256,128]{2,1,0:T(8,128)} %s_hbm.1), custom_call_target="tpu_custom_call" | custom-call | tf_op jit(solution)/shard_map/pallas_call | solution.py:585
  30.1 3.1 %copy.4 = f32[16,256,128]{2,1,0:T(8,128)} copy(f32[16,256,128]{2,1,0:T(8,128)} %shard_map.28) | data formatting | bytes 4194304

commit v8 on v7

--- a/solution.py
+++ b/solution.py
@@ -41,10 +41,11 @@
         pl.semaphore_signal(barrier, inc=1, device_id=device, device_id_type=MESH)
 
     for e in range(2):
-        greet({"gy": y_to[e]})
-        greet({"gz": z_to[e]})
         for d in range(2):
             greet({"gy": y_to[e], "gz": z_to[d]})
+    for e in range(2):
+        greet({"gz": z_to[e]})
+        greet({"gy": y_to[e]})
 
         @pl.when(has[e])
         def _():

time: 33.3 us -> 33.3 us (level)
  no operation moved by 1% of the time
where the time goes in v8:
time: 33.3 us; the launch traced here: 33.2 us
  Pallas kernels  30.1 us (90%)
  local copies, waits for them, and re-layouts  3.11 us (9%)
    pallas_call x1, Pallas kernels, on_device(): pl.pallas_call(functools.partial(kernel, sizes), out_shape=jax.ShapeDtype...  30.1 us
    unnamed x1, local copies, waits for them, and re-layouts  3.11 us

profile of v8, /device:TPU:1, one launch (start us, length us, event | category | flops | bytes accessed | tf_op | source)
XLA Modules:
  0.0 33.2 jit_solution(13734422406713788494)
XLA Ops:
  0.0 30.1 %shard_map.28 = f32[16,256,128]{2,1,0:T(8,128)} custom-call(f32[16,256,128]{2,1,0:T(8,128)} %f_hbm.1, f32[16,256,128]{2,1,0:T(8,128)} %s_hbm.1), custom_call_target="tpu_custom_call" | custom-call | tf_op jit(solution)/shard_map/pallas_call | solution.py:586
  30.1 3.1 %copy.4 = f32[16,256,128]{2,1,0:T(8,128)} copy(f32[16,256,128]{2,1,0:T(8,128)} %shard_map.28) | data formatting | bytes 4194304
